TPU v7x, 64 devices: a 2x2x8 block of a 4x4x8 slice. The times are simulated.
64 devices in a mesh: dp: 4 (over x, y), sp: 16 (over z, core).
Axes of the slice: x: 2, y: 2, z: 8, core: 2. Of those that a mesh axis runs over, the one named last changes fastest.
The devices are a block of a 4x4x8 slice.
Arguments:
- tokens: bfloat16 [8192, 4096], P(('dp', 'sp')), parts along dimension 0
- w_query: bfloat16 [4096, 8192], replicated
- w_key: bfloat16 [4096, 512], replicated
- w_value: bfloat16 [4096, 512], replicated
- w_out: bfloat16 [8192, 4096], replicated
- w_gate: bfloat16 [4096, 4096], replicated
- w_up: bfloat16 [4096, 4096], replicated
- w_down: bfloat16 [4096, 4096], replicated
- w_router: bfloat16 [4096, 128], replicated
- expert_ids: int32 [8192, 8], P(('dp', 'sp')), parts along dimension 0
Outputs:
- output 1: bfloat16 [8192, 4096], P(('dp', 'sp')), parts along dimension 0
- output 2: bfloat16 [512, 256, 4096], P(('dp', 'sp')), parts along dimension 0
There are 4 independent parts. A program takes and returns all parts, laid end to end along the dimension named above; an argument that names none is the same for every part.
All inputs are finite; a program needn't handle non-finite values.
Results may differ from a plain program's by a relative error of at most 0.00603084.
Values are sent between devices in bfloat16 or wider.
A program may use at most 768 MiB of HBM per device.

v0:
```python
import math
import jax
import jax.numpy as jnp
from jax import lax
from jax.sharding import PartitionSpec as P

HEAD_DIM = 128


def query_block(n_rows, n_heads, seq_len):
    blk_rows = n_rows
    while blk_rows > 8 and blk_rows * n_heads * seq_len > 2 ** 24:
        blk_rows = blk_rows // 2
    return blk_rows


def head_attention(q_rows, k_all, v_all, kv_loc, q_offset):
    n_rows = q_rows.shape[0]
    seq_len = k_all.shape[0]
    q_per_kv = q_rows.shape[1] // (kv_loc * HEAD_DIM)
    blk_rows = query_block(n_rows, kv_loc * q_per_kv, seq_len)
    q_blocks = q_rows.reshape(n_rows // blk_rows, blk_rows, kv_loc, q_per_kv, HEAD_DIM)
    keys_heads = k_all.reshape(seq_len, kv_loc, HEAD_DIM)
    values_heads = v_all.reshape(seq_len, kv_loc, HEAD_DIM)
    key_pos = jnp.arange(seq_len, dtype=jnp.int32)
    inv_scale = 1.0 / math.sqrt(HEAD_DIM)

    def one_block(blk_args):
        q_blk, q_start = blk_args
        scores = jnp.einsum('qkgd,skd->kgqs', q_blk, keys_heads, preferred_element_type=jnp.float32) * inv_scale
        query_pos = q_start + jnp.arange(blk_rows, dtype=jnp.int32)
        scores = jnp.where(query_pos[:, None] >= key_pos[None, :], scores, -jnp.inf)
        attn_probs = jax.nn.softmax(scores, axis=-1).astype(jnp.bfloat16)
        blk_out = jnp.einsum('kgqs,skd->qkgd', attn_probs, values_heads, preferred_element_type=jnp.float32)
        return blk_out.astype(jnp.bfloat16).reshape(blk_rows, kv_loc * q_per_kv * HEAD_DIM)

    starts = q_offset + jnp.arange(n_rows // blk_rows, dtype=jnp.int32) * blk_rows
    return lax.map(one_block, (q_blocks, starts)).reshape(n_rows, kv_loc * q_per_kv * HEAD_DIM)


def shared_expert(hidden, w_gate, w_up, w_down):
    gate_act = jnp.dot(hidden, w_gate, preferred_element_type=jnp.float32)
    up_act = jnp.dot(hidden, w_up, preferred_element_type=jnp.float32)
    swiglu = (jax.nn.silu(gate_act) * up_act).astype(jnp.bfloat16)
    return (hidden.astype(jnp.float32) + jnp.dot(swiglu, w_down, preferred_element_type=jnp.float32)).astype(jnp.bfloat16)


def dispatch_rows(hidden, w_router, expert_ids, capacity):
    tok_rows, hidden_dim = hidden.shape
    n_experts = w_router.shape[1]
    top_k = expert_ids.shape[1]
    logits = jnp.dot(hidden, w_router, preferred_element_type=jnp.float32)
    gate_vals = jax.nn.sigmoid(jnp.take_along_axis(logits, expert_ids, axis=1)).reshape(-1)
    pair_expert = expert_ids.reshape(-1)
    onehot = (pair_expert[:, None] == jnp.arange(n_experts, dtype=jnp.int32)[None, :]).astype(jnp.int32)
    slot_rank = jnp.sum((jnp.cumsum(onehot, axis=0) - onehot) * onehot, axis=1)
    n_slots = n_experts * capacity
    dest_row = jnp.where(slot_rank < capacity, pair_expert * capacity + slot_rank, n_slots)
    pair_token = jnp.arange(tok_rows * top_k, dtype=jnp.int32) // top_k
    slot_token = jax.ops.segment_sum(pair_token, dest_row, num_segments=n_slots)
    slot_gate = jax.ops.segment_sum(gate_vals, dest_row, num_segments=n_slots)
    gathered = jnp.take(hidden, slot_token, axis=0)
    return (gathered.astype(jnp.float32) * slot_gate[:, None]).astype(jnp.bfloat16).reshape(n_experts, capacity, hidden_dim)


def head_columns(proj, kv_heads, n_grp):
    if n_grp <= kv_heads:
        return proj
    tok_rows = proj.shape[0]
    repeated = jnp.repeat(proj.reshape(tok_rows, kv_heads, HEAD_DIM), n_grp // kv_heads, axis=1)
    return repeated.reshape(tok_rows, n_grp * HEAD_DIM)


def solution(mesh):
    n_grp = mesh.shape['sp']
    row_spec = P(('dp', 'sp'), None)
    buf_spec = P(('dp', 'sp'), None, None)
    replicated = P()

    def local_step(tokens, w_query, w_key, w_value, w_out, w_gate, w_up, w_down, w_router, expert_ids):
        tok_rows = tokens.shape[0]
        kv_heads = w_key.shape[1] // HEAD_DIM
        n_experts = w_router.shape[1]
        top_k = expert_ids.shape[1]
        capacity = max(2, (tok_rows * top_k // n_experts) * 2)
        kv_loc = max(kv_heads // n_grp, 1)
        queries = jnp.dot(tokens, w_query, preferred_element_type=jnp.float32).astype(jnp.bfloat16)
        keys_loc = jnp.dot(tokens, w_key, preferred_element_type=jnp.float32).astype(jnp.bfloat16)
        values_loc = jnp.dot(tokens, w_value, preferred_element_type=jnp.float32).astype(jnp.bfloat16)
        q_all = lax.all_to_all(queries, 'sp', 1, 0, tiled=True)
        k_all = lax.all_to_all(head_columns(keys_loc, kv_heads, n_grp), 'sp', 1, 0, tiled=True)
        v_all = lax.all_to_all(head_columns(values_loc, kv_heads, n_grp), 'sp', 1, 0, tiled=True)
        attn_heads = head_attention(q_all, k_all, v_all, kv_loc, 0)
        attn_loc = lax.all_to_all(attn_heads, 'sp', 0, 1, tiled=True)
        hidden = (tokens.astype(jnp.float32) + jnp.dot(attn_loc, w_out, preferred_element_type=jnp.float32)).astype(jnp.bfloat16)
        hidden_out = shared_expert(hidden, w_gate, w_up, w_down)
        send_buf = dispatch_rows(hidden, w_router, expert_ids, capacity)
        expert_buf = lax.all_to_all(send_buf, 'sp', 0, 1, tiled=True)
        return hidden_out, expert_buf

    return jax.shard_map(local_step, mesh=mesh, in_specs=(row_spec, replicated, replicated, replicated, replicated, replicated, replicated, replicated, replicated, row_spec), out_specs=(row_spec, buf_spec), check_vma=False)
```

profile of v0, /device:TPU:21, one launch (start us, length us, event | category | flops | bytes accessed | tf_op | source)
XLA Modules:
  0.0 727.3 jit_solution(6410616442342161150)
XLA Ops:
  5.0 10.7 %all-to-all-start = ((bf16[128,16,128]{0,2,1:T(8,128)(2,1)}), bf16[128,16,128]{0,2,1:T(8,128)(2,1)S(1)}, u32[]{:S(2)}, u32[]{:S(2)}) async-start(bf16[128,16,128]{0,2,1:T(8,128)(2,1)} %bitcast.1), calls=%async_computation | async-start | bytes 1048576 | tf_op jit(solution)/shard_map/all_to_all | solution.py:92
  15.7 25.3 %convolution_convert_fusion = bf16[128,8192]{1,0:T(8,128)(2,1)} fusion(bf16[128,4096]{1,0:T(8,128)(2,1)} %param.10, bf16[4096,8192]{1,0:T(8,128)(2,1)} %param.11), kind=kOutput, calls=%fused_computation.13 | convolution fusion | flops 8590983168 | bytes 70254592 | tf_op jit(solution)/shard_map/dot_general | solution.py:87
  41.0 4.1 copy.72
  45.1 7.2 all-to-all-start.2
  55.3 45.8 %all-to-all-done.2 = bf16[128,16,512]{0,2,1:T(8,128)(2,1)} async-done(((bf16[128,16,512]{0,2,1:T(8,128)(2,1)}), bf16[128,16,512]{0,2,1:T(8,128)(2,1)}, u32[]{:S(2)}, u32[]{:S(2)}) %all-to-all-start.2) | async-done | bytes 2097184 | tf_op jit(solution)/shard_map/all_to_all | solution.py:90
  102.0 5.4 all-to-all-start.1
  107.4 4.1 iota_compare_fusion
  118.2 5.5 all-to-all-done.1
  123.7 27.6 %fusion.1 = (f32[4,2048]{1,0:T(4,128)S(1)}, f32[2048,2048,4]{1,0,2:T(8,128)}) fusion(pred[2048,2048]{0,1:T(8,128)(4,1)} %iota_compare_fusion, bf16[2048,128,1]{1,0,2:T(8,128)(2,1)} %bitcast.6, bf16[2048,4,128]{0,2,1:T(8,128)(2,1)} %reshape.151), kind=kOutput, calls=%fused_computation.8 | convolution fusion | flops 4345290752 | bytes 73957376 | tf_op jit(solution)/shard_map/while/body/eval_jaxpr/qkgd,skd->kgqs/dot_general | solution.py:30
  151.3 23.0 %fusion = f32[4,2048]{1,0:T(4,128)S(1)} fusion(f32[2048,2048,4]{1,0,2:T(8,128)} %get-tuple-element.15, f32[4,2048]{1,0:T(4,128)S(1)} %get-tuple-element.14, pred[2048,2048]{0,1:T(8,128)(4,1)} %iota_compare_fusion), kind=kLoop, calls=%fused_computation.7 | loop fusion | flops 67100672 | bytes 71368704 | tf_op jit(solution)/shard_map/while/body/eval_jaxpr/reduce_sum | solution.py:33
  174.3 27.7 %fusion.7 = bf16[128,4,2048]{2,0,1:T(8,128)(2,1)} fusion(bf16[2048,128,1]{0,1,2:T(8,128)(2,1)S(1)} %copy-done.3, f32[4,2048]{1,0:T(4,128)S(1)} %fusion, f32[4,2048]{1,0:T(4,128)S(1)} %get-tuple-element.14, f32[2048,2048,4]{1,0,2:T(8,128)} %get-tuple-element.15, pred[2048,2048]{0,1:T(8,128)(4,1)} %iota_compare_fusion), kind=kOutput, calls=%fused_computation.20 | convolution fusion | flops 4379901952 | bytes 73990144 | tf_op jit(solution)/shard_map/while/body/eval_jaxpr/kgqs,skd->qkgd/dot_general | solution.py:34
  206.1 4.5 all-to-all-start.3
  212.3 5.9 scatter_custom_fusion
  218.4 40.6 %all-to-all-done.3 = bf16[16,128,512]{1,2,0:T(8,128)(2,1)} async-done(((bf16[16,128,512]{1,2,0:T(8,128)(2,1)}), bf16[16,128,512]{1,2,0:T(8,128)(2,1)}, u32[]{:S(2)}, u32[]{:S(2)}) %all-to-all-start.3) | async-done | bytes 2097184 | tf_op jit(solution)/shard_map/all_to_all | solution.py:94
  259.0 24.5 %fusion.4 = bf16[128,4096]{1,0:T(8,128)(2,1)S(1)} fusion(bf16[128,8192]{0,1:T(8,128)(2,1)} %bitcast.15, bf16[8192,4096]{1,0:T(8,128)(2,1)} %param.14, bf16[128,4096]{1,0:T(8,128)(2,1)S(1)} %copy-done.2), kind=kOutput, calls=%fused_computation.17 | convolution fusion | flops 8591507456 | bytes 71303168 | tf_op jit(solution)/shard_map/dot_general | solution.py:95
  283.5 14.0 %gather_fusion = bf16[2048,4096]{1,0:T(8,128)(2,1)} fusion(bf16[128,4096]{1,0:T(8,128)(2,1)S(1)} %fusion.4, s32[2048]{0:T(1024)S(1)} %fusion.22), kind=kCustom, calls=%fused_computation | custom fusion | bytes 33562624 | tf_op jit(solution)/shard_map/jit(_take)/gather | solution.py:62
  297.9 6.8 gather_fusion.1
  305.1 5.9 scatter_custom_fusion.1
  311.1 16.7 %multiply_convert_fusion = bf16[128,16,4096]{2,1,0:T(8,128)(2,1)} fusion(f32[128,16]{1,0:T(8,128)S(1)} %mul.52, bf16[128,16,4096]{2,1,0:T(8,128)(2,1)} %bitcast.91, pred[128,16]{1,0:T(8,128)(4,1)S(1)} %broadcast_in_dim.66), kind=kLoop, calls=%fused_computation.11 | loop fusion | flops 33554432 | bytes 33564672 | tf_op jit(solution)/shard_map/convert_element_type | solution.py:63
  327.8 5.6 all-to-all-start.4
  333.4 14.3 %fusion.33 = f32[128,4096]{1,0:T(8,128)} fusion(bf16[128,4096]{1,0:T(8,128)(2,1)S(1)} %fusion.4, bf16[4096,4096]{1,0:T(8,128)(2,1)} %param.15), kind=kOutput, calls=%fused_computation.63 | convolution fusion | flops 4294967296 | bytes 36700160 | tf_op jit(solution)/shard_map/dot_general | solution.py:42
  347.7 25.7 %fusion.5 = bf16[128,4096]{1,0:T(8,128)(2,1)} fusion(bf16[4096,4096]{1,0:T(8,128)(2,1)} %param.17, bf16[128,4096]{1,0:T(8,128)(2,1)S(1)} %fusion.4, bf16[4096,4096]{1,0:T(8,128)(2,1)} %param.16, f32[128,4096]{1,0:T(8,128)} %fusion.33), kind=kOutput, calls=%fused_computation.18 | convolution fusion | flops 8594653184 | bytes 71303168 | tf_op jit(solution)/shard_map/dot_general | solution.py:45
  373.4 339.8 %all-to-all-done.4 = bf16[128,16,4096]{2,1,0:T(8,128)(2,1)} async-done(((bf16[128,16,4096]{2,1,0:T(8,128)(2,1)}), bf16[128,16,4096]{2,1,0:T(8,128)(2,1)}, u32[]{:S(2)}, u32[]{:S(2)}) %all-to-all-start.4) | async-done | bytes 16777248 | tf_op jit(solution)/shard_map/all_to_all | solution.py:98
  713.2 14.1 %copy.68 = bf16[16,8,16,4096]{3,2,0,1:T(8,128)(2,1)} copy(bf16[16,8,16,4096]{3,2,1,0:T(8,128)(2,1)} %bitcast.23) | data formatting | bytes 33554432 | tf_op jit(solution)/shard_map/all_to_all | solution.py:98
  (52 shorter events, 21.5 us)
Async XLA Ops:
  0.6 296.9 %copy-start = (bf16[4096,128]{1,0:T(8,128)(2,1)S(1)}, bf16[4096,128]{1,0:T(8,128)(2,1)}, u32[]{:S(2)}) copy-start(bf16[4096,128]{1,0:T(8,128)(2,1)} %param.18) | copy-start | bytes 3145732
  5.0 40.1 %all-to-all-start = ((bf16[128,16,128]{0,2,1:T(8,128)(2,1)}), bf16[128,16,128]{0,2,1:T(8,128)(2,1)S(1)}, u32[]{:S(2)}, u32[]{:S(2)}) async-start(bf16[128,16,128]{0,2,1:T(8,128)(2,1)} %bitcast.1), calls=%async_computation | async-start | bytes 1048576 | tf_op jit(solution)/shard_map/all_to_all | solution.py:92
  15.7 36.6 %copy-start.1 = (bf16[128,4096]{1,0:T(8,128)(2,1)S(1)}, bf16[128,4096]{1,0:T(8,128)(2,1)}, u32[]{:S(2)}) copy-start(bf16[128,4096]{1,0:T(8,128)(2,1)} %param.10) | copy-start | bytes 3145732
  45.1 56.0 %all-to-all-start.2 = ((bf16[128,16,512]{0,2,1:T(8,128)(2,1)}), bf16[128,16,512]{0,2,1:T(8,128)(2,1)}, u32[]{:S(2)}, u32[]{:S(2)}) async-start(bf16[128,16,512]{0,2,1:T(8,128)(2,1)} %bitcast.93), calls=%async_computation.2 | async-start | bytes 4194304 | tf_op jit(solution)/shard_map/all_to_all | solution.py:90
  102.0 21.7 %all-to-all-start.1 = ((bf16[128,16,128]{2,0,1:T(8,128)(2,1)}), bf16[128,16,128]{2,0,1:T(8,128)(2,1)}, u32[]{:S(2)}, u32[]{:S(2)}) async-start(bf16[128,16,128]{2,0,1:T(8,128)(2,1)} %bitcast.3), calls=%async_computation.1 | async-start | bytes 1048576 | tf_op jit(solution)/shard_map/all_to_all | solution.py:91
  151.2 23.0 %copy-start.3 = (bf16[2048,128,1]{0,1,2:T(8,128)(2,1)S(1)}, bf16[2048,128,1]{0,1,2:T(8,128)(2,1)}, u32[]{:S(2)}) copy-start(bf16[2048,128,1]{0,1,2:T(8,128)(2,1)} %reshape.194) | copy-start | bytes 1572868
  174.3 36.4 %copy-start.4 = (s32[128,8]{0,1:T(8,128)S(1)}, s32[128,8]{0,1:T(8,128)}, u32[]{:S(2)}) copy-start(s32[128,8]{0,1:T(8,128)} %param.19) | copy-start | bytes 12292
  202.0 57.0 %copy-start.2 = (bf16[128,4096]{1,0:T(8,128)(2,1)S(1)}, bf16[128,4096]{1,0:T(8,128)(2,1)}, u32[]{:S(2)}) copy-start(bf16[128,4096]{1,0:T(8,128)(2,1)} %param.10) | copy-start | bytes 3145732
  206.1 52.8 %all-to-all-start.3 = ((bf16[16,128,512]{1,2,0:T(8,128)(2,1)}), bf16[16,128,512]{1,2,0:T(8,128)(2,1)}, u32[]{:S(2)}, u32[]{:S(2)}) async-start(bf16[16,128,512]{1,2,0:T(8,128)(2,1)} %copy.59), calls=%async_computation.3 | async-start | bytes 4194304 | tf_op jit(solution)/shard_map/all_to_all | solution.py:94
  327.8 385.3 %all-to-all-start.4 = ((bf16[128,16,4096]{2,1,0:T(8,128)(2,1)}), bf16[128,16,4096]{2,1,0:T(8,128)(2,1)}, u32[]{:S(2)}, u32[]{:S(2)}) async-start(bf16[128,16,4096]{2,1,0:T(8,128)(2,1)} %multiply_convert_fusion), calls=%async_computation.4 | async-start | bytes 33554432 | tf_op jit(solution)/shard_map/all_to_all | solution.py:98
where the time goes:
time: 728 us; the launch traced here: 727 us
  waiting for transfers between devices  432 us (59%)
  matrix products  152 us (21%)
  other arithmetic  56.4 us (8%)
  local copies, waits for them, and re-layouts  53.1 us (7%)
  starting transfers between devices  33.5 us (5%)
    all_to_all x1, waiting for transfers between devices, local_step(): expert_buf = lax.all_to_all(send_buf, 'sp', 0, 1, tiled=True)  340 us
    all_to_all x1, waiting for transfers between devices, local_step(): q_all = lax.all_to_all(queries, 'sp', 1, 0, tiled=True)  45.8 us
    all_to_all x1, waiting for transfers between devices, local_step(): attn_loc = lax.all_to_all(attn_heads, 'sp', 0, 1, tiled=True)  40.6 us
    dot_general x1, matrix products, one_block(): jnp.einsum('kgqs,skd->qkgd', attn_probs, values_heads, preferred_element_...  27.7 us
    dot_general x1, matrix products, one_block(): jnp.einsum('qkgd,skd->kgqs', q_blk, keys_heads, preferred_element_type=jn...  27.6 us
    dot_general x1, matrix products, shared_expert(): jnp.dot(swiglu, w_down, preferred_element_type=jnp.float32)  25.7 us
    dot_general x1, matrix products, local_step(): jnp.dot(tokens, w_query, preferred_element_type=jnp.float32)  25.3 us
    dot_general x1, matrix products, local_step(): jnp.dot(attn_loc, w_out, preferred_element_type=jnp.float32)  24.5 us
  transfers between devices with their start and end apart: 5, of which 4 were waited for; matrix products, arithmetic and copies ran while one was open for 12% of the time, Pallas kernels for 0%

commit v1 on v0

v1 whole, which is shorter than its diff:
```python
import functools
import math
import jax
import jax.numpy as jnp
from jax import lax
from jax.experimental import pallas as pl
from jax.experimental.pallas import tpu as pltpu
from jax.sharding import PartitionSpec as P

HEAD_DIM = 128
NT = (((1,), (1,)), ((), ()))


def attention_body(chunk, rows, me_ref, q_ref, k_ref, v_ref, o_ref, m_ref, l_ref, acc_ref):
    tok = q_ref.shape[0]
    heads = q_ref.shape[1] // HEAD_DIM
    per = rows // tok
    me = me_ref[0]
    factor = math.log2(math.e) / math.sqrt(HEAD_DIM)
    m_ref[...] = jnp.full(m_ref.shape, -jnp.inf, jnp.float32)
    l_ref[...] = jnp.zeros(l_ref.shape, jnp.float32)
    acc_ref[...] = jnp.zeros(acc_ref.shape, jnp.float32)

    def step(start, masked):
        keys = k_ref[pl.ds(start, chunk), :]
        vals = v_ref[pl.ds(start, chunk), :]
        for g in range(heads // per):
            q = jnp.concatenate([q_ref[:, (g * per + i) * HEAD_DIM:(g * per + i + 1) * HEAD_DIM] for i in range(per)], axis=0)
            s = lax.dot_general(q, keys, NT, preferred_element_type=jnp.float32) * factor
            if masked:
                pos = me * tok + lax.rem(lax.broadcasted_iota(jnp.int32, s.shape, 0), tok)
                key = start + lax.broadcasted_iota(jnp.int32, s.shape, 1)
                s = jnp.where(key <= pos, s, -jnp.inf)
            sl = pl.ds(g * rows, rows)
            m_old = m_ref[sl, :1]
            m_new = jnp.maximum(m_old, jnp.max(s, axis=1, keepdims=True))
            p = jnp.exp2(s - m_new)
            alpha = jnp.exp2(m_old - m_new)
            part = p[:, :128]
            for i in range(1, chunk // 128):
                part = part + p[:, i * 128:(i + 1) * 128]
            l_ref[sl, :] = l_ref[sl, :] * alpha + part
            acc_ref[sl, :] = acc_ref[sl, :] * alpha + jnp.dot(p.astype(jnp.bfloat16), vals, preferred_element_type=jnp.float32)
            m_ref[sl, :] = jnp.broadcast_to(m_new, (rows, 128))

    full = (me * tok) // chunk

    @pl.loop(0, full)
    def _(c):
        step(pl.multiple_of(c * chunk, chunk), False)

    step(pl.multiple_of(full * chunk, chunk), True)
    for h in range(heads):
        sl = pl.ds(h * tok, tok)
        total = jnp.sum(l_ref[sl, :], axis=1, keepdims=True)
        o_ref[:, h * HEAD_DIM:(h + 1) * HEAD_DIM] = (acc_ref[sl, :] / total).astype(o_ref.dtype)


def attention(me, queries, kv_all, chunk=512, rows=512):
    tok, width = queries.shape
    seq = kv_all.shape[0]
    kv_heads = kv_all.shape[1] // (2 * HEAD_DIM)
    cols = width // kv_heads
    all_rows = tok * cols // HEAD_DIM
    return pl.pallas_call(
        functools.partial(attention_body, chunk, rows),
        out_shape=jax.ShapeDtypeStruct((tok, width), jnp.bfloat16),
        grid_spec=pltpu.PrefetchScalarGridSpec(
            num_scalar_prefetch=1,
            grid=(kv_heads,),
            in_specs=[
                pl.BlockSpec((tok, cols), lambda i, me: (0, i)),
                pl.BlockSpec((seq, HEAD_DIM), lambda i, me: (0, i)),
                pl.BlockSpec((seq, HEAD_DIM), lambda i, me: (0, kv_heads + i)),
            ],
            out_specs=pl.BlockSpec((tok, cols), lambda i, me: (0, i)),
            scratch_shapes=[
                pltpu.VMEM((all_rows, 128), jnp.float32),
                pltpu.VMEM((all_rows, 128), jnp.float32),
                pltpu.VMEM((all_rows, 128), jnp.float32),
            ],
        ),
        cost_estimate=pl.CostEstimate(flops=4 * tok * width * seq, bytes_accessed=4 * tok * width + 2 * kv_all.size, transcendentals=0),
        compiler_params=pltpu.CompilerParams(vmem_limit_bytes=48 * 2 ** 20),
        name='attention',
    )(me, queries, kv_all, kv_all)


def expand_body(cap, rank_ref, gate_ref, h_ref, out_ref):
    n_loc, tok = rank_ref.shape[1:]
    shape = (n_loc, cap, tok)
    slot = lax.broadcasted_iota(jnp.int32, shape, 1).astype(jnp.float32)
    hit = jnp.broadcast_to(rank_ref[0][:, None, :], shape) == slot
    sel = jnp.where(hit, 1.0, 0.0)
    gate = jnp.sum(sel * jnp.broadcast_to(gate_ref[0][:, None, :], shape), axis=2, keepdims=True)
    sel = sel.reshape(n_loc * cap, tok).astype(jnp.bfloat16)
    gate = gate.reshape(n_loc * cap, 1)
    rows = jnp.dot(sel, h_ref[...], preferred_element_type=jnp.float32)
    out_ref[...] = (rows * gate).astype(out_ref.dtype).reshape(out_ref.shape)


def expand(h_all, rank, gate, cap):
    n_src, n_loc, tok = rank.shape
    width = h_all.shape[1]
    return pl.pallas_call(
        functools.partial(expand_body, cap),
        out_shape=jax.ShapeDtypeStruct((n_loc, n_src * cap, width), jnp.bfloat16),
        grid=(n_src,),
        in_specs=[
            pl.BlockSpec((1, n_loc, tok), lambda s: (s, 0, 0)),
            pl.BlockSpec((1, n_loc, tok), lambda s: (s, 0, 0)),
            pl.BlockSpec((tok, width), lambda s: (s, 0)),
        ],
        out_specs=pl.BlockSpec((n_loc, cap, width), lambda s: (0, s, 0)),
        cost_estimate=pl.CostEstimate(flops=2 * n_src * n_loc * cap * tok * width, bytes_accessed=4 * h_all.size, transcendentals=0),
        name='expand',
    )(rank, gate, h_all)


def slot_ranks(expert_ids, n_experts):
    tok = expert_ids.shape[0]
    chosen = jnp.any(expert_ids[:, :, None] == jnp.arange(n_experts, dtype=jnp.int32), axis=1)
    earlier = jnp.tril(jnp.ones((tok, tok), jnp.bfloat16), -1)
    rank = jnp.dot(earlier, chosen.astype(jnp.bfloat16), preferred_element_type=jnp.float32)
    return jnp.where(chosen, rank, -1.0).T


def solution(mesh):
    row_spec = P(('dp', 'sp'), None)
    buf_spec = P(('dp', 'sp'), None, None)
    replicated = P()

    def local_step(tokens, w_query, w_key, w_value, w_out, w_gate, w_up, w_down, w_router, expert_ids):
        f32, bf16 = jnp.float32, jnp.bfloat16
        tok = tokens.shape[0]
        n_grp = mesh.shape['sp']
        n_experts = w_router.shape[1]
        n_loc = n_experts // n_grp
        cap = max(2, (tok * expert_ids.shape[1] // n_experts) * 2)
        me = lax.axis_index('sp').astype(jnp.int32).reshape(1)
        keys = jnp.dot(tokens, w_key, preferred_element_type=f32).astype(bf16)
        values = jnp.dot(tokens, w_value, preferred_element_type=f32).astype(bf16)
        kv_all = lax.all_gather(jnp.concatenate([keys, values], axis=1), 'sp', axis=0, tiled=True)
        queries = jnp.dot(tokens, w_query, preferred_element_type=f32).astype(bf16)
        attn = attention(me, queries, kv_all)
        hidden = (tokens.astype(f32) + jnp.dot(attn, w_out, preferred_element_type=f32)).astype(bf16)
        h_all = lax.all_gather(hidden, 'sp', axis=0, tiled=True)
        rank = slot_ranks(expert_ids, n_experts)
        gate = jax.nn.sigmoid(jnp.dot(hidden, w_router, preferred_element_type=f32)).T
        table = jnp.concatenate([rank.reshape(n_grp, n_loc, tok), gate.reshape(n_grp, n_loc, tok)], axis=1)
        table = lax.all_to_all(table, 'sp', 0, 0, tiled=True)
        gate_act = jnp.dot(hidden, w_gate, preferred_element_type=f32)
        up_act = jnp.dot(hidden, w_up, preferred_element_type=f32)
        swiglu = (jax.nn.silu(gate_act) * up_act).astype(bf16)
        hidden_out = (hidden.astype(f32) + jnp.dot(swiglu, w_down, preferred_element_type=f32)).astype(bf16)
        expert_buf = expand(h_all, table[:, :n_loc], table[:, n_loc:], cap)
        return hidden_out, expert_buf

    return jax.shard_map(local_step, mesh=mesh, in_specs=(row_spec,) + (replicated,) * 8 + (row_spec,), out_specs=(row_spec, buf_spec), check_vma=False)
```

time: 728 us -> 264 us (0.36)
  waiting for transfers between devices: 432 us -> 64.6 us
  matrix products: 152 us -> 94.6 us
  other arithmetic: 56.4 us -> 1.64 us
  local copies, waits for them, and re-layouts: 53.1 us -> 3.16 us
  Pallas kernels: 0 us -> 41.2 us
  between operations: 0.91 us -> 14.2 us
  starting transfers between devices: 33.5 us -> 44.2 us
    all_to_all x5 -> x1, waiting for transfers between devices: 432 us -> 0.01 us  [local_step(): table = lax.all_to_all(table, 'sp', 0, 0, tiled=True)]
    all_gather x0 -> x2, waiting for transfers between devices: none -> 64.5 us  [the longest x1 45.1 us: local_step(): h_all = lax.all_gather(hidden, 'sp', axis=0, tiled=True)]
    dot_general x9 -> x8, matrix products: 152 us -> 94.6 us  [the longest x1 25.7 us: local_step(): jnp.dot(swiglu, w_down, preferred_element_type=f32)]
    pallas_call x0 -> x2, Pallas kernels: none -> 41.2 us  [the longest x1 21 us: attention(): pl.pallas_call(functools.partial(attention_body, chunk, rows), out_shape=...]
    reduce_sum x2 -> x0, other arithmetic: 23.3 us -> none  [the longest x1 23 us: one_block(): attn_probs = jax.nn.softmax(scores, axis=-1).astype(jnp.bfloat16)]
    all_to_all x5 -> x0, local copies, waits for them, and re-layouts: 23.3 us -> none  [the longest x1 14.1 us: local_step(): expert_buf = lax.all_to_all(send_buf, 'sp', 0, 1, tiled=True)]
    gather x6 -> x0, local copies, waits for them, and re-layouts: 21.1 us -> none  [the longest x1 14 us: dispatch_rows(): gathered = jnp.take(hidden, slot_token, axis=0)]
    convert_element_type x1 -> x0, other arithmetic: 16.7 us -> none  [dispatch_rows(): (gathered.astype(jnp.float32) * slot_gate[:, None]).astype(jnp.bfloat16)]
  transfers between devices with their start and end apart: 5 -> 3, of which waited for: 4 -> 2; matrix products, arithmetic and copies ran while one was open for 12% -> 26% of each run, Pallas kernels for 0% -> 0%
where the time goes in v1:
time: 264 us
  matrix products  94.6 us (36%)
  waiting for transfers between devices  64.6 us (24%)
  starting transfers between devices  44.2 us (17%)
  Pallas kernels  41.2 us (16%)
  between operations  14.2 us (5%)
  local copies, waits for them, and re-layouts  3.16 us (1%)
    all_gather x1, waiting for transfers between devices, local_step(): h_all = lax.all_gather(hidden, 'sp', axis=0, tiled=True)  45.1 us
    all_to_all x1, starting transfers between devices, local_step(): table = lax.all_to_all(table, 'sp', 0, 0, tiled=True)  44.1 us
    dot_general x1, matrix products, local_step(): jnp.dot(swiglu, w_down, preferred_element_type=f32)  25.7 us
    dot_general x1, matrix products, local_step(): queries = jnp.dot(tokens, w_query, preferred_element_type=f32).astype(bf16)  24.3 us
    dot_general x1, matrix products, local_step(): jnp.dot(attn, w_out, preferred_element_type=f32)  24.2 us
    pallas_call x1, Pallas kernels, attention(): pl.pallas_call(functools.partial(attention_body, chunk, rows), out_shape=...  21 us
    pallas_call x1, Pallas kernels, expand(): pl.pallas_call(functools.partial(expand_body, cap), out_shape=jax.ShapeDt...  20.2 us
    all_gather x1, waiting for transfers between devices, local_step(): lax.all_gather(jnp.concatenate([keys, values], axis=1), 'sp', axis=0, til...  19.5 us
  transfers between devices with their start and end apart: 3, of which 2 were waited for; matrix products, arithmetic and copies ran while one was open for 26% of the time, Pallas kernels for 0%

profile of v1, /device:TPU:21, one launch (start us, length us, event | category | flops | bytes accessed | tf_op | source)
XLA Modules:
  0.0 263.6 jit_solution(15066824943672357668)
XLA Ops:
  7.2 0.1 all-gather.3.cloned.1.call-start
  7.3 3.4 %convolution_convert_fusion.2 = bf16[128,512]{1,0:T(8,128)(2,1)S(1)} fusion(bf16[128,4096]{1,0:T(8,128)(2,1)} %param.10, bf16[4096,512]{1,0:T(8,128)(2,1)} %param.12), kind=kOutput, calls=%fused_computation.13 | convolution fusion | flops 536936448 | bytes 5373952 | tf_op jit(solution)/shard_map/dot_general | solution.py:141
  10.7 0.7 copy-done.5
  11.4 0.8 convolution_convert_fusion.1
  12.1 0.7 pad_maximum_fusion
  12.9 0.1 all-gather.3.cloned.1.call-update
  12.9 0.1 all-gather.5.cloned.1.call-start
  13.0 24.3 %convolution_convert_fusion.q_ref = bf16[128,8192]{1,0:T(8,128)(2,1)} fusion(bf16[128,4096]{1,0:T(8,128)(2,1)S(1)} %copy-done.4, bf16[4096,8192]{1,0:T(8,128)(2,1)} %param.11), kind=kOutput, calls=%fused_computation | convolution fusion | flops 8590983168 | bytes 70254592 | tf_op jit(solution)/shard_map/dot_general | solution.py:144
  37.3 19.5 %all-gather.3.cloned.1.call-done.k_ref.v_ref = bf16[2048,1024]{1,0:T(8,128)(2,1)} async-done(((bf16[128,1024]{1,0:T(8,128)(2,1)}), bf16[2048,1024]{1,0:T(8,128)(2,1)}) %all-gather.3.cloned.1.call-update) | async-done | bytes 4194320 | tf_op jit(solution)/shard_map/all_gather | solution.py:143
  56.8 1.6 copy-done.2
  58.4 21.0 %attention.1 = bf16[128,8192]{1,0:T(8,128)(2,1)S(1)} custom-call(s32[1]{0:T(128)} %bitcast.me_ref, bf16[128,8192]{1,0:T(8,128)(2,1)S(1)} %copy-done.2, bf16[2048,1024]{1,0:T(8,128)(2,1)} %all-gather.3.cloned.1.call-done.k_ref.v_ref, bf16[2048,1024]{1,0:T(8,128)(2,1)} %all-gather.3.cloned.1.call-done.k_ref.v_ref), custom_call_target="tpu_custom_call" | custom-call | flops 8589934592 | bytes 8388608 | tf_op jit(solution)/shard_map/attention/pallas_call | solution.py:65
  79.4 24.2 %fusion = bf16[128,4096]{1,0:T(8,128)(2,1)} fusion(bf16[128,8192]{1,0:T(8,128)(2,1)S(1)} %attention.1, bf16[8192,4096]{1,0:T(8,128)(2,1)} %param.14, bf16[128,4096]{1,0:T(8,128)(2,1)} %param.10), kind=kOutput, calls=%fused_computation.4 | convolution fusion | flops 8591507456 | bytes 71303168 | tf_op jit(solution)/shard_map/dot_general | solution.py:146
  103.7 0.1 copy.13
  103.8 0.3 fusion.14
  104.0 0.1 copy.14
  104.1 0.2 fusion.8
  104.4 1.8 fusion.12
  106.1 0.7 pad_maximum_fusion.1
  106.8 44.1 %all-to-all-start = ((f32[16,16,128]{2,1,0:T(8,128)}), f32[16,16,128]{2,1,0:T(8,128)S(1)}, u32[]{:S(2)}, u32[]{:S(2)}) async-start(f32[16,16,128]{2,1,0:T(8,128)} %pad_maximum_fusion.1), calls=%async_computation | async-start | bytes 262144 | tf_op jit(solution)/shard_map/all_to_all | solution.py:151
  150.9 14.2 %fusion.25 = f32[128,4096]{1,0:T(8,128)} fusion(bf16[128,4096]{1,0:T(8,128)(2,1)S(1)} %copy-done.3, bf16[4096,4096]{1,0:T(8,128)(2,1)} %param.15), kind=kOutput, calls=%fused_computation.37 | convolution fusion | flops 4294967296 | bytes 36700160 | tf_op jit(solution)/shard_map/dot_general | solution.py:152
  165.1 25.7 %fusion.1 = bf16[128,4096]{1,0:T(8,128)(2,1)} fusion(bf16[4096,4096]{1,0:T(8,128)(2,1)} %param.17, bf16[128,4096]{1,0:T(8,128)(2,1)S(1)} %copy-done.3, bf16[4096,4096]{1,0:T(8,128)(2,1)} %param.16, f32[128,4096]{1,0:T(8,128)} %fusion.25), kind=kOutput, calls=%fused_computation.5 | convolution fusion | flops 8594653184 | bytes 71303168 | tf_op jit(solution)/shard_map/dot_general | solution.py:155
  190.9 0.6 fusion.24
  191.5 45.1 %all-gather.5.cloned.1.call-done.h_ref = bf16[2048,4096]{1,0:T(8,128)(2,1)} async-done(((bf16[128,4096]{1,0:T(8,128)(2,1)}), bf16[2048,4096]{1,0:T(8,128)(2,1)}) %all-gather.5.cloned.1.call-update) | async-done | bytes 16777232 | tf_op jit(solution)/shard_map/all_gather | solution.py:147
  236.6 20.2 %expand.1 = bf16[8,256,4096]{2,1,0:T(8,128)(2,1)} custom-call(f32[16,8,128]{2,1,0:T(8,128)} %get-tuple-element.3.rank_ref, f32[16,8,128]{2,1,0:T(8,128)} %get-tuple-element.2.gate_ref, bf16[2048,4096]{1,0:T(8,128)(2,1)} %all-gather.5.cloned.1.call-done.h_ref), custom_call_target="tpu_custom_call" | custom-call | flops 2147483648 | bytes 33554432 | tf_op jit(solution)/shard_map/expand/pallas_call | solution.py:105
  (15 shorter events, 0.1 us)
Async XLA Ops:
  7.2 97.2 %copy-start = (bf16[4096,128]{1,0:T(8,128)(2,1)S(1)}, bf16[4096,128]{1,0:T(8,128)(2,1)}, u32[]{:S(2)}) copy-start(bf16[4096,128]{1,0:T(8,128)(2,1)} %param.18) | copy-start | bytes 3145732
  7.2 3.5 %copy-start.4 = (bf16[128,4096]{1,0:T(8,128)(2,1)S(1)}, bf16[128,4096]{1,0:T(8,128)(2,1)}, u32[]{:S(2)}) copy-start(bf16[128,4096]{1,0:T(8,128)(2,1)} %param.10) | copy-start | bytes 3145732
  7.2 49.6 %all-gather.3.cloned.1.call-start = ((), (), s32[]{:S(2)}) async-start(), calls=%async_computation.1 | async-start | bytes 4456448 | tf_op jit(solution)/shard_map/all_gather | solution.py:143
  7.3 4.1 %copy-start.5 = (bf16[4096,512]{1,0:T(8,128)(2,1)S(1)}, bf16[4096,512]{1,0:T(8,128)(2,1)}, u32[]{:S(2)}) copy-start(bf16[4096,512]{1,0:T(8,128)(2,1)} %param.13) | copy-start | bytes 12582916
  12.9 223.6 %all-gather.5.cloned.1.call-start = ((), (), s32[]{:S(2)}) async-start(), calls=%async_computation.2 | async-start | bytes 17825792 | tf_op jit(solution)/shard_map/all_gather | solution.py:147
  56.8 1.6 copy-start.2
  79.4 24.3 %copy-start.6 = (s32[128,8]{0,1:T(8,128)S(1)}, s32[128,8]{0,1:T(8,128)}, u32[]{:S(2)}) copy-start(s32[128,8]{0,1:T(8,128)} %param.19) | copy-start | bytes 12292
  103.6 47.3 %copy-start.3 = (bf16[128,4096]{1,0:T(8,128)(2,1)S(1)}, bf16[128,4096]{1,0:T(8,128)(2,1)}, u32[]{:S(2)}) copy-start(bf16[128,4096]{1,0:T(8,128)(2,1)} %fusion) | copy-start | bytes 3145732
  106.8 84.1 %all-to-all-start = ((f32[16,16,128]{2,1,0:T(8,128)}), f32[16,16,128]{2,1,0:T(8,128)S(1)}, u32[]{:S(2)}, u32[]{:S(2)}) async-start(f32[16,16,128]{2,1,0:T(8,128)} %pad_maximum_fusion.1), calls=%async_computation | async-start | bytes 262144 | tf_op jit(solution)/shard_map/all_to_all | solution.py:151
  236.6 20.2 %copy-start.1 = (bf16[4096,128]{1,0:T(8,128)(2,1)S(1)}, bf16[4096,128]{1,0:T(8,128)(2,1)}, u32[]{:S(2)}) copy-start(bf16[4096,128]{1,0:T(8,128)(2,1)} %param.18) | copy-start | bytes 3145732
Sparse Core Ops, SparseCore 0:
  13.0 43.6 all-gather.2
  103.8 132.7 all-gather.4

commit v2 on v1

--- a/solution.py
+++ b/solution.py
@@ -9,6 +9,8 @@
 
 HEAD_DIM = 128
 NT = (((1,), (1,)), ((), ()))
+MESH = pl.DeviceIdType.MESH
+LAG = 3
 
 
 def attention_body(chunk, rows, me_ref, q_ref, k_ref, v_ref, o_ref, m_ref, l_ref, acc_ref):
@@ -86,35 +88,295 @@
     )(me, queries, kv_all, kv_all)
 
 
-def expand_body(cap, rank_ref, gate_ref, h_ref, out_ref):
-    n_loc, tok = rank_ref.shape[1:]
-    shape = (n_loc, cap, tok)
-    slot = lax.broadcasted_iota(jnp.int32, shape, 1).astype(jnp.float32)
-    hit = jnp.broadcast_to(rank_ref[0][:, None, :], shape) == slot
-    sel = jnp.where(hit, 1.0, 0.0)
-    gate = jnp.sum(sel * jnp.broadcast_to(gate_ref[0][:, None, :], shape), axis=2, keepdims=True)
-    sel = sel.reshape(n_loc * cap, tok).astype(jnp.bfloat16)
-    gate = gate.reshape(n_loc * cap, 1)
-    rows = jnp.dot(sel, h_ref[...], preferred_element_type=jnp.float32)
-    out_ref[...] = (rows * gate).astype(out_ref.dtype).reshape(out_ref.shape)
-
-
-def expand(h_all, rank, gate, cap):
-    n_src, n_loc, tok = rank.shape
-    width = h_all.shape[1]
+class Ring:
+    def __init__(self, n, buf, up_send, down_send, ring_recv, mate_send, mate_recv):
+        self.n, self.len, self.chunks = n, n // 2, buf.shape[1]
+        self.half = self.chunks // 2
+        self.buf, self.up_send, self.down_send = buf, up_send, down_send
+        self.ring_recv, self.mate_send, self.mate_recv = ring_recv, mate_send, mate_recv
+        self.me = lax.axis_index('sp')
+        self.mate = self.me + 1 - 2 * lax.rem(self.me, 2)
+        self.up = lax.rem(self.me + 2, n)
+        self.down = lax.rem(self.me + n - 2, n)
+
+    def barrier(self):
+        sem = pltpu.get_barrier_semaphore()
+        for i in range(1, self.n):
+            pl.semaphore_signal(sem, inc=1, device_id={'sp': lax.rem(self.me + i, self.n)}, device_id_type=MESH)
+        pl.semaphore_wait(sem, self.n - 1)
+
+    def owner(self, delta, base=None):
+        return lax.rem((self.me if base is None else base) + 2 * delta, self.n)
+
+    def copy(self, delta, j, send_sem, recv_sem, target):
+        piece = self.buf.at[self.owner(delta), j]
+        return pltpu.make_async_remote_copy(src_ref=piece, dst_ref=piece, send_sem=send_sem, recv_sem=recv_sem,
+                                            device_id={'sp': target}, device_id_type=MESH)
+
+    def up_copy(self, dist, j):
+        delta = lax.rem(self.len - dist, self.len)
+        return self.copy(delta, j, self.up_send.at[dist, j], self.ring_recv.at[lax.rem(delta + self.len - 1, self.len), j], self.up)
+
+    def down_copy(self, dist, j):
+        return self.copy(dist, j, self.down_send.at[dist, j], self.ring_recv.at[dist + 1, j], self.down)
+
+    def mate_copy(self, delta, j):
+        return self.copy(delta, j, self.mate_send.at[delta, j], self.mate_recv.at[delta, j], self.mate)
+
+    def wait_ring(self, delta, j):
+        self.copy(delta, j, self.mate_send.at[delta, j], self.ring_recv.at[delta, j], self.mate).wait_recv()
+
+    def wait_mate(self, delta, j):
+        piece = self.buf.at[self.owner(delta, self.mate), j]
+        pltpu.make_async_remote_copy(src_ref=piece, dst_ref=piece, send_sem=self.mate_send.at[delta, j], recv_sem=self.mate_recv.at[delta, j],
+                                     device_id={'sp': self.mate}, device_id_type=MESH).wait_recv()
+
+    def send_own(self, j):
+        self.up_copy(0, j).start()
+        self.down_copy(0, j).start()
+        self.mate_copy(0, j).start()
+
+    def step(self, r):
+        dist, j = r // self.chunks + 1, lax.rem(r, self.chunks)
+        last = 2 * self.chunks
+        self.wait_ring(self.len - dist, j)
+
+        @pl.when(r < last + self.half)
+        def _():
+            self.up_copy(dist, j).start()
+
+        self.mate_copy(self.len - dist, j).start()
+        self.wait_ring(dist, j)
+
+        @pl.when((r < last) | (r >= last + self.half))
+        def _():
+            self.down_copy(dist, j).start()
+
+        self.mate_copy(dist, j).start()
+
+    def far_step(self, i):
+        far = self.len // 2
+        for j in (i, i + self.half):
+            self.wait_ring(far, j)
+            self.mate_copy(far, j).start()
+
+    def drain(self):
+        far = self.len // 2
+
+        @pl.loop(0, self.chunks)
+        def _(j):
+            for dist in range(far):
+                @pl.when((dist < far - 1) | (j < self.half))
+                def _(dist=dist):
+                    self.up_copy(dist, j).wait_send()
+
+                @pl.when((dist < far - 1) | (j >= self.half))
+                def _(dist=dist):
+                    self.down_copy(dist, j).wait_send()
+            for delta in range(self.len):
+                self.mate_copy(delta, j).wait_send()
+
+
+def ring_scratch(n, chunks):
+    length, far = n // 2, n // 4
+    dma = pltpu.SemaphoreType.DMA
+    return [dma((far, chunks)), dma((far, chunks)), dma((length, chunks)), dma((length, chunks)), dma((length, chunks))]
+
+
+class Tiles:
+    def __init__(self, slots, sems, groups):
+        self.slots, self.sems, self.groups = slots, sems, groups
+        self.depth, self.total = slots.shape[0], groups[-1][0]
+
+    def copy(self, tile, slot):
+        return pltpu.make_async_copy(tile, self.slots.at[slot], self.sems.at[slot])
+
+    def start(self, t):
+        first = 0
+        for end, pick in self.groups:
+            @pl.when((t >= first) & (t < end))
+            def _(first=first, pick=pick):
+                for cond, tile in pick(t - first):
+                    if cond is None:
+                        self.copy(tile, lax.rem(t, self.depth)).start()
+                    else:
+                        @pl.when(cond)
+                        def _(tile=tile):
+                            self.copy(tile, lax.rem(t, self.depth)).start()
+            first = end
+
+    def prime(self):
+        for t in range(self.depth - 1):
+            self.start(jnp.int32(t))
+
+    def take(self, t):
+        self.start(t + self.depth - 1)
+        slot = lax.rem(t, self.depth)
+        self.copy(self.groups[0][1](0)[0][1], slot).wait()
+        return self.slots.at[slot]
+
+
+def columns(j, width):
+    return pl.ds(pl.multiple_of(j * width, width), width)
+
+
+def tail_body(n, cap, o_ref, x_ref, rank_ref, router_ref, wo_ref, wg_ref, wu_ref, wd_ref, y_ref, e_ref,
+              buf, row_ref, act_ref, slots, table_out, table_in, sems, table_send, table_recv, *ring_sems):
+    f32, bf16 = jnp.float32, jnp.bfloat16
+    ring = Ring(n, buf, *ring_sems)
+    me = ring.me
+    chunks, tok, width = buf.shape[1:]
+    depth = slots.shape[1]
+    parts = o_ref.shape[1] // depth
+    n_loc = rank_ref.shape[0] // n
+    tiles = Tiles(slots, sems, (
+        (parts * chunks, lambda t: [(None, wo_ref.at[columns(lax.rem(t, parts), depth), columns(t // parts, width)])]),
+        ((parts + 2) * chunks, lambda t: [(lax.rem(t, 2) == 0, wg_ref.at[:, columns(t // 2, width)]),
+                                          (lax.rem(t, 2) == 1, wu_ref.at[:, columns(t // 2, width)])]),
+        ((parts + 3) * chunks, lambda t: [(None, wd_ref.at[:, columns(t, width)])]),
+    ))
+    tiles.prime()
+    ring.barrier()
+
+    @pl.loop(0, chunks)
+    def _(j):
+        acc = x_ref[:, columns(j, width)].astype(f32)
+        part = None
+        for i in range(parts):
+            prod = jnp.dot(o_ref[:, i * depth:(i + 1) * depth], tiles.take(parts * j + i)[...], preferred_element_type=f32)
+            part = prod if part is None else part + prod
+        h = (acc + part).astype(bf16)
+        buf[me, j] = h
+        row_ref[:, columns(j, width)] = h
+        ring.send_own(j)
+
+        @pl.when(j >= LAG)
+        def _():
+            ring.step(j - LAG)
+
+    gate = jax.nn.sigmoid(jnp.dot(row_ref[...], router_ref[...], preferred_element_type=f32)).T
+    for d in range(n):
+        table_out[d, :n_loc] = rank_ref[d * n_loc:(d + 1) * n_loc]
+        table_out[d, n_loc:] = gate[d * n_loc:(d + 1) * n_loc]
+    table_in[me] = table_out[me]
+
+    def table_copy(i):
+        dst = lax.rem(me + i, n)
+        return pltpu.make_async_remote_copy(src_ref=table_out.at[dst], dst_ref=table_in.at[me], send_sem=table_send.at[i], recv_sem=table_recv.at[i],
+                                            device_id={'sp': dst}, device_id_type=MESH)
+
+    def table_arrival(i):
+        src = lax.rem(me + n - i, n)
+        return pltpu.make_async_remote_copy(src_ref=table_out.at[src], dst_ref=table_in.at[src], send_sem=table_send.at[i], recv_sem=table_recv.at[i],
+                                            device_id={'sp': src}, device_id_type=MESH)
+
+    for i in range(1, n):
+        table_copy(i).start()
+
+    base = parts * chunks
+
+    @pl.loop(0, chunks)
+    def _(j):
+        h = row_ref[...]
+        g = jnp.dot(h, tiles.take(base + 2 * j)[...], preferred_element_type=f32)
+        u = jnp.dot(h, tiles.take(base + 2 * j + 1)[...], preferred_element_type=f32)
+        act_ref[:, columns(j, width)] = (g * jax.nn.sigmoid(g) * u).astype(bf16)
+        ring.step(j + chunks - LAG)
+
+    base += 2 * chunks
+
+    @pl.loop(0, chunks)
+    def _(j):
+        y = jnp.dot(act_ref[...], tiles.take(base + j)[...], preferred_element_type=f32)
+        y_ref[:, columns(j, width)] = (row_ref[:, columns(j, width)].astype(f32) + y).astype(bf16)
+
+        @pl.when(lax.rem(j, 2) == 1)
+        def _():
+            ring.step(2 * chunks - LAG + j // 2)
+
+    for i in range(1, n):
+        table_arrival(i).wait_recv()
+
+    def expand(src, js):
+        shape = (n_loc, cap, tok)
+        table = table_in[src]
+        slot = lax.broadcasted_iota(jnp.int32, shape, 1).astype(f32)
+        sel = jnp.where(jnp.broadcast_to(table[:n_loc][:, None, :], shape) == slot, 1.0, 0.0)
+        scale = jnp.sum(sel * jnp.broadcast_to(table[n_loc:][:, None, :], shape), axis=2, keepdims=True).reshape(n_loc * cap, 1)
+        sel = sel.reshape(n_loc * cap, tok).astype(bf16)
+        for j in js:
+            rows = jnp.dot(sel, buf[src, j], preferred_element_type=f32) * scale
+            e_ref[:, pl.ds(pl.multiple_of(src * cap, cap), cap), columns(j, width)] = rows.astype(bf16).reshape(n_loc, cap, width)
+
+    def expand_pair(delta):
+        expand(ring.owner(delta), range(chunks))
+
+        @pl.loop(0, chunks)
+        def _(j):
+            ring.wait_mate(delta, j)
+
+        expand(ring.owner(delta, ring.mate), range(chunks))
+
+    done = 2 * chunks - LAG + chunks // 2
+    length, far = n // 2, n // 4
+    near = 2 * far - 3
+
+    @pl.loop(0, 3 * chunks - done)
+    def _(k):
+        ring.step(done + k)
+
+        @pl.when(k < near)
+        def _():
+            expand_pair(jnp.where(lax.rem(k, 2) == 1, length - (k + 1) // 2, k // 2))
+
+    @pl.loop(0, chunks // 2)
+    def _(i):
+        ring.far_step(i)
+
+        @pl.when(i < 2)
+        def _():
+            expand_pair(jnp.where(i == 0, far + 1, far - 1))
+
+    @pl.loop(0, chunks // 2)
+    def _(i):
+        js = (i, i + chunks // 2)
+        expand(ring.owner(far), js)
+        for j in js:
+            ring.wait_mate(far, j)
+        expand(ring.owner(far, ring.mate), js)
+
+    ring.drain()
+    for i in range(1, n):
+        table_copy(i).wait_send()
+
+
+def tail(n, cap, attn, tokens, rank, w_router, w_out, w_gate, w_up, w_down, chunks=8, depth=4):
+    tok, hidden = tokens.shape
+    width = hidden // chunks
+    n_loc = rank.shape[0] // n
+    vmem = pl.BlockSpec(memory_space=pltpu.VMEM)
+    hbm = pl.BlockSpec(memory_space=pl.ANY)
+    dma = pltpu.SemaphoreType.DMA
+    weights = w_out.size + w_gate.size + w_up.size + w_down.size
     return pl.pallas_call(
-        functools.partial(expand_body, cap),
-        out_shape=jax.ShapeDtypeStruct((n_loc, n_src * cap, width), jnp.bfloat16),
-        grid=(n_src,),
-        in_specs=[
-            pl.BlockSpec((1, n_loc, tok), lambda s: (s, 0, 0)),
-            pl.BlockSpec((1, n_loc, tok), lambda s: (s, 0, 0)),
-            pl.BlockSpec((tok, width), lambda s: (s, 0)),
-        ],
-        out_specs=pl.BlockSpec((n_loc, cap, width), lambda s: (0, s, 0)),
-        cost_estimate=pl.CostEstimate(flops=2 * n_src * n_loc * cap * tok * width, bytes_accessed=4 * h_all.size, transcendentals=0),
-        name='expand',
-    )(rank, gate, h_all)
+        functools.partial(tail_body, n, cap),
+        out_shape=(jax.ShapeDtypeStruct((tok, hidden), jnp.bfloat16),
+                   jax.ShapeDtypeStruct((n_loc, n * cap, hidden), jnp.bfloat16)),
+        in_specs=[vmem] * 4 + [hbm] * 4,
+        out_specs=(vmem, vmem),
+        scratch_shapes=[
+            pltpu.VMEM((n, chunks, tok, width), jnp.bfloat16),
+            pltpu.VMEM((tok, hidden), jnp.bfloat16),
+            pltpu.VMEM((tok, hidden), jnp.bfloat16),
+            pltpu.VMEM((depth, hidden, width), jnp.bfloat16),
+            pltpu.VMEM((n, 2 * n_loc, tok), jnp.float32),
+            pltpu.VMEM((n, 2 * n_loc, tok), jnp.float32),
+            dma((depth,)), dma((n,)), dma((n,)),
+        ] + ring_scratch(n, chunks),
+        cost_estimate=pl.CostEstimate(flops=2 * tok * weights, bytes_accessed=2 * weights, transcendentals=0),
+        compiler_params=pltpu.CompilerParams(vmem_limit_bytes=67043328, collective_id=0, has_side_effects=True),
+        name='tail',
+    )(attn, tokens, rank, w_router, w_out, w_gate, w_up, w_down)
 
 
 def slot_ranks(expert_ids, n_experts):
@@ -135,7 +397,6 @@
         tok = tokens.shape[0]
         n_grp = mesh.shape['sp']
         n_experts = w_router.shape[1]
-        n_loc = n_experts // n_grp
         cap = max(2, (tok * expert_ids.shape[1] // n_experts) * 2)
         me = lax.axis_index('sp').astype(jnp.int32).reshape(1)
         keys = jnp.dot(tokens, w_key, preferred_element_type=f32).astype(bf16)
@@ -143,17 +404,8 @@
         kv_all = lax.all_gather(jnp.concatenate([keys, values], axis=1), 'sp', axis=0, tiled=True)
         queries = jnp.dot(tokens, w_query, preferred_element_type=f32).astype(bf16)
         attn = attention(me, queries, kv_all)
-        hidden = (tokens.astype(f32) + jnp.dot(attn, w_out, preferred_element_type=f32)).astype(bf16)
-        h_all = lax.all_gather(hidden, 'sp', axis=0, tiled=True)
         rank = slot_ranks(expert_ids, n_experts)
-        gate = jax.nn.sigmoid(jnp.dot(hidden, w_router, preferred_element_type=f32)).T
-        table = jnp.concatenate([rank.reshape(n_grp, n_loc, tok), gate.reshape(n_grp, n_loc, tok)], axis=1)
-        table = lax.all_to_all(table, 'sp', 0, 0, tiled=True)
-        gate_act = jnp.dot(hidden, w_gate, preferred_element_type=f32)
-        up_act = jnp.dot(hidden, w_up, preferred_element_type=f32)
-        swiglu = (jax.nn.silu(gate_act) * up_act).astype(bf16)
-        hidden_out = (hidden.astype(f32) + jnp.dot(swiglu, w_down, preferred_element_type=f32)).astype(bf16)
-        expert_buf = expand(h_all, table[:, :n_loc], table[:, n_loc:], cap)
+        hidden_out, expert_buf = tail(n_grp, cap, attn, tokens, rank, w_router, w_out, w_gate, w_up, w_down)
         return hidden_out, expert_buf
 
     return jax.shard_map(local_step, mesh=mesh, in_specs=(row_spec,) + (replicated,) * 8 + (row_spec,), out_specs=(row_spec, buf_spec), check_vma=False)

time: 264 us -> 245 us (0.928)
  Pallas kernels: 41.2 us -> 164 us
  matrix products: 94.6 us -> 28 us
  waiting for transfers between devices: 64.6 us -> 19.5 us
  starting transfers between devices: 44.2 us -> 0.06 us
  local copies, waits for them, and re-layouts: 3.16 us -> 18.5 us
    pallas_call x1, Pallas kernels: 20.2 us -> 143 us  [tail(): pl.pallas_call(functools.partial(tail_body, n, cap), out_shape=(jax.Shape...]
    dot_general x4 -> x0, matrix products: 65.9 us -> none  [the longest x1 25.7 us: local_step(): jnp.dot(swiglu, w_down, preferred_element_type=f32)]
    all_gather x1 -> x0, waiting for transfers between devices: 45.1 us -> none  [local_step(): h_all = lax.all_gather(hidden, 'sp', axis=0, tiled=True)]
    all_to_all x1 -> x0, starting transfers between devices: 44.1 us -> none  [local_step(): table = lax.all_to_all(table, 'sp', 0, 0, tiled=True)]
    unnamed x15 -> x11, local copies, waits for them, and re-layouts: 2.41 us -> 18.4 us
  transfers between devices with their start and end apart: 3 -> 1, of which waited for: 2 -> 1; matrix products, arithmetic and copies ran while one was open for 26% -> 10% of each run, Pallas kernels for 0% -> 0%
where the time goes in v2:
time: 245 us
  Pallas kernels  164 us (67%)
  matrix products  28 us (11%)
  waiting for transfers between devices  19.5 us (8%)
  local copies, waits for them, and re-layouts  18.5 us (8%)
  between operations  14.2 us (6%)
    pallas_call x1, Pallas kernels, tail(): pl.pallas_call(functools.partial(tail_body, n, cap), out_shape=(jax.Shape...  143 us
    dot_general x1, matrix products, local_step(): queries = jnp.dot(tokens, w_query, preferred_element_type=f32).astype(bf16)  23 us
    pallas_call x1, Pallas kernels, attention(): pl.pallas_call(functools.partial(attention_body, chunk, rows), out_shape=...  21 us
    all_gather x1, waiting for transfers between devices, local_step(): lax.all_gather(jnp.concatenate([keys, values], axis=1), 'sp', axis=0, til...  19.5 us
    unnamed x11, local copies, waits for them, and re-layouts  18.4 us
  transfers between devices with their start and end apart: 1, of which 1 were waited for; matrix products, arithmetic and copies ran while one was open for 10% of the time, Pallas kernels for 0%

profile of v2, /device:TPU:21, one launch (start us, length us, event | category | flops | bytes accessed | tf_op | source)
XLA Modules:
  0.0 244.8 jit_solution(6115897145580809974)
XLA Ops:
  7.2 0.0 copy-start.1
  7.2 0.1 all-gather.2.cloned.1.call-start
  7.3 0.0 copy-start.2
  7.3 3.4 %convolution_convert_fusion.2 = bf16[128,512]{1,0:T(8,128)(2,1)S(1)} fusion(bf16[128,4096]{1,0:T(8,128)(2,1)} %x_ref.1, bf16[4096,512]{1,0:T(8,128)(2,1)} %param.12), kind=kOutput, calls=%fused_computation.2 | convolution fusion | flops 536936448 | bytes 5373952 | tf_op jit(solution)/shard_map/dot_general | solution.py:402
  10.6 0.0 copy-done.1
  10.7 0.6 copy-done.2
  11.3 0.0 copy-start.3
  11.3 0.8 convolution_convert_fusion.1
  12.1 0.7 pad_maximum_fusion
  12.8 0.1 all-gather.2.cloned.1.call-update
  12.8 0.0 copy-done.3
  12.9 0.1 copy.13
  13.0 0.3 fusion
  13.2 0.1 copy.14
  13.3 0.8 convolution_select_fusion.rank_ref
  14.2 23.0 %convolution_convert_fusion.q_ref = bf16[128,8192]{1,0:T(8,128)(2,1)S(1)} fusion(bf16[128,4096]{1,0:T(8,128)(2,1)S(1)} %copy-done.1, bf16[4096,8192]{1,0:T(8,128)(2,1)} %param.11), kind=kOutput, calls=%fused_computation | convolution fusion | flops 8590983168 | bytes 70254592 | tf_op jit(solution)/shard_map/dot_general | solution.py:405
  37.2 19.5 %all-gather.2.cloned.1.call-done.k_ref.v_ref = bf16[2048,1024]{1,0:T(8,128)(2,1)} async-done(((bf16[128,1024]{1,0:T(8,128)(2,1)}), bf16[2048,1024]{1,0:T(8,128)(2,1)}) %all-gather.2.cloned.1.call-update) | async-done | bytes 4194320 | tf_op jit(solution)/shard_map/all_gather | solution.py:404
  56.7 21.0 %attention.1.o_ref = bf16[128,8192]{1,0:T(8,128)(2,1)S(1)} custom-call(s32[1]{0:T(128)} %bitcast.me_ref, bf16[128,8192]{1,0:T(8,128)(2,1)S(1)} %convolution_convert_fusion.q_ref, bf16[2048,1024]{1,0:T(8,128)(2,1)} %all-gather.2.cloned.1.call-done.k_ref.v_ref, bf16[2048,1024]{1,0:T(8,128)(2,1)} %all-gather.2.cloned.1.call-done.k_ref.v_ref), custom_call_target="tpu_custom_call" | custom-call | flops 8589934592 | bytes 8388608 | tf_op jit(solution)/shard_map/attention/pallas_call | solution.py:67
  77.7 0.0 copy-start
  77.7 1.3 copy-done
  79.0 142.6 %tail.1 = (bf16[128,4096]{1,0:T(8,128)(2,1)}, bf16[8,256,4096]{2,1,0:T(8,128)(2,1)}) custom-call(bf16[128,8192]{1,0:T(8,128)(2,1)} %copy-done, bf16[128,4096]{1,0:T(8,128)(2,1)} %x_ref.1, f32[128,128]{1,0:T(8,128)} %convolution_select_fusion.rank_ref, bf16[4096,128]{1,0:T(8,128)(2,1)} %router_ref.1, bf16[8192,4096]{1,0:T(8,128)(2,1)} %wo_ref.1, ...), custom_call_target="tpu_custom_call" | custom-call | flops 21474836480 | bytes 167772160 | tf_op jit(solution)/shard_map/tail/pallas_call | solution.py:361
  221.6 2.3 copy.18
  223.9 14.1 %copy.19 = bf16[8,256,4096]{2,1,0:T(8,128)(2,1)} copy(bf16[8,256,4096]{2,1,0:T(8,128)(2,1)} %get-tuple-element.5) | data formatting | bytes 33554432
  (1 shorter events, 0.0 us)
Async XLA Ops:
  7.2 3.5 %copy-start.1 = (bf16[128,4096]{1,0:T(8,128)(2,1)S(1)}, bf16[128,4096]{1,0:T(8,128)(2,1)}, u32[]{:S(2)}) copy-start(bf16[128,4096]{1,0:T(8,128)(2,1)} %x_ref.1) | copy-start | bytes 3145732
  7.2 49.5 %all-gather.2.cloned.1.call-start = ((), (), s32[]{:S(2)}) async-start(), calls=%async_computation | async-start | bytes 4456448 | tf_op jit(solution)/shard_map/all_gather | solution.py:404
  7.3 4.0 %copy-start.2 = (bf16[4096,512]{1,0:T(8,128)(2,1)S(1)}, bf16[4096,512]{1,0:T(8,128)(2,1)}, u32[]{:S(2)}) copy-start(bf16[4096,512]{1,0:T(8,128)(2,1)} %param.13) | copy-start | bytes 12582916
  11.3 1.6 copy-start.3
  77.7 1.3 copy-start
Sparse Core Ops, SparseCore 0:
  13.0 43.6 all-gather.1

commit v3 on v2

--- a/solution.py
+++ b/solution.py
@@ -13,55 +13,56 @@
 LAG = 3
 
 
-def attention_body(chunk, rows, me_ref, q_ref, k_ref, v_ref, o_ref, m_ref, l_ref, acc_ref):
+def attention_body(chunk, rows, me_ref, q_ref, k_ref, v_ref, o_ref, m_ref, l_ref, acc_ref, bias_ref):
     tok = q_ref.shape[0]
     heads = q_ref.shape[1] // HEAD_DIM
     per = rows // tok
+    blocks = chunk // tok
     me = me_ref[0]
     factor = math.log2(math.e) / math.sqrt(HEAD_DIM)
+    full = (me * tok) // chunk
     m_ref[...] = jnp.full(m_ref.shape, -jnp.inf, jnp.float32)
     l_ref[...] = jnp.zeros(l_ref.shape, jnp.float32)
     acc_ref[...] = jnp.zeros(acc_ref.shape, jnp.float32)
-
-    def step(start, masked):
-        keys = k_ref[pl.ds(start, chunk), :]
-        vals = v_ref[pl.ds(start, chunk), :]
+    pos = me * tok - full * chunk + lax.broadcasted_iota(jnp.int32, bias_ref.shape, 0)
+    key = lax.broadcasted_iota(jnp.int32, bias_ref.shape, 1)
+    bias_ref[...] = jnp.where(key <= pos, 0.0, -jnp.inf)
+
+    def step(c, masked):
+        keys = k_ref[pl.ds(c * blocks, blocks), 0].reshape(chunk, HEAD_DIM)
+        vals = v_ref[pl.ds(c * blocks, blocks), 0].reshape(chunk, HEAD_DIM)
         for g in range(heads // per):
             q = jnp.concatenate([q_ref[:, (g * per + i) * HEAD_DIM:(g * per + i + 1) * HEAD_DIM] for i in range(per)], axis=0)
             s = lax.dot_general(q, keys, NT, preferred_element_type=jnp.float32) * factor
             if masked:
-                pos = me * tok + lax.rem(lax.broadcasted_iota(jnp.int32, s.shape, 0), tok)
-                key = start + lax.broadcasted_iota(jnp.int32, s.shape, 1)
-                s = jnp.where(key <= pos, s, -jnp.inf)
+                s = (s.reshape(per, tok, chunk) + bias_ref[...][None]).reshape(rows, chunk)
             sl = pl.ds(g * rows, rows)
-            m_old = m_ref[sl, :1]
+            m_old = m_ref[sl, :]
             m_new = jnp.maximum(m_old, jnp.max(s, axis=1, keepdims=True))
-            p = jnp.exp2(s - m_new)
+            p = jnp.exp2(s - m_new[:, :1])
             alpha = jnp.exp2(m_old - m_new)
             part = p[:, :128]
             for i in range(1, chunk // 128):
                 part = part + p[:, i * 128:(i + 1) * 128]
             l_ref[sl, :] = l_ref[sl, :] * alpha + part
             acc_ref[sl, :] = acc_ref[sl, :] * alpha + jnp.dot(p.astype(jnp.bfloat16), vals, preferred_element_type=jnp.float32)
-            m_ref[sl, :] = jnp.broadcast_to(m_new, (rows, 128))
-
-    full = (me * tok) // chunk
+            m_ref[sl, :] = m_new
 
     @pl.loop(0, full)
     def _(c):
-        step(pl.multiple_of(c * chunk, chunk), False)
-
-    step(pl.multiple_of(full * chunk, chunk), True)
+        step(c, False)
+
+    step(full, True)
     for h in range(heads):
         sl = pl.ds(h * tok, tok)
         total = jnp.sum(l_ref[sl, :], axis=1, keepdims=True)
-        o_ref[:, h * HEAD_DIM:(h + 1) * HEAD_DIM] = (acc_ref[sl, :] / total).astype(o_ref.dtype)
+        o_ref[:, h * HEAD_DIM:(h + 1) * HEAD_DIM] = (acc_ref[sl, :] * (1.0 / total)).astype(o_ref.dtype)
 
 
 def attention(me, queries, kv_all, chunk=512, rows=512):
     tok, width = queries.shape
-    seq = kv_all.shape[0]
-    kv_heads = kv_all.shape[1] // (2 * HEAD_DIM)
+    n_src, _, _, kv_width = kv_all.shape
+    kv_heads = kv_width // HEAD_DIM
     cols = width // kv_heads
     all_rows = tok * cols // HEAD_DIM
     return pl.pallas_call(
@@ -72,18 +73,19 @@
             grid=(kv_heads,),
             in_specs=[
                 pl.BlockSpec((tok, cols), lambda i, me: (0, i)),
-                pl.BlockSpec((seq, HEAD_DIM), lambda i, me: (0, i)),
-                pl.BlockSpec((seq, HEAD_DIM), lambda i, me: (0, kv_heads + i)),
+                pl.BlockSpec((n_src, 1, tok, HEAD_DIM), lambda i, me: (0, 0, 0, i)),
+                pl.BlockSpec((n_src, 1, tok, HEAD_DIM), lambda i, me: (0, 1, 0, i)),
             ],
             out_specs=pl.BlockSpec((tok, cols), lambda i, me: (0, i)),
             scratch_shapes=[
                 pltpu.VMEM((all_rows, 128), jnp.float32),
                 pltpu.VMEM((all_rows, 128), jnp.float32),
                 pltpu.VMEM((all_rows, 128), jnp.float32),
+                pltpu.VMEM((tok, chunk), jnp.float32),
             ],
         ),
-        cost_estimate=pl.CostEstimate(flops=4 * tok * width * seq, bytes_accessed=4 * tok * width + 2 * kv_all.size, transcendentals=0),
-        compiler_params=pltpu.CompilerParams(vmem_limit_bytes=48 * 2 ** 20),
+        cost_estimate=pl.CostEstimate(flops=4 * tok * width * n_src * tok, bytes_accessed=4 * tok * width + 2 * kv_all.size, transcendentals=0),
+        compiler_params=pltpu.CompilerParams(vmem_limit_bytes=40 * 2 ** 20),
         name='attention',
     )(me, queries, kv_all, kv_all)
 
@@ -220,8 +222,69 @@
     return pl.ds(pl.multiple_of(j * width, width), width)
 
 
+def front_body(n, x_ref, wk_ref, wv_ref, wq_ref, q_ref, kv_ref, buf, slots, sems, out_sem, *ring_sems):
+    ring = Ring(n, buf, *ring_sems)
+    width = slots.shape[2]
+    count = wq_ref.shape[1] // width
+    tiles = Tiles(slots, sems, (
+        (1, lambda t: [(None, wk_ref)]),
+        (2, lambda t: [(None, wv_ref)]),
+        (2 + count, lambda t: [(None, wq_ref.at[:, columns(t, width)])]),
+    ))
+    tiles.prime()
+    ring.barrier()
+    for c in range(2):
+        buf[ring.me, c] = jnp.dot(x_ref[...], tiles.take(jnp.int32(c))[...], preferred_element_type=jnp.float32).astype(jnp.bfloat16)
+        ring.send_own(jnp.int32(c))
+
+    steps = 3 * ring.chunks
+
+    @pl.loop(0, count)
+    def _(j):
+        q_ref[:, columns(j, width)] = jnp.dot(x_ref[...], tiles.take(j + 2)[...], preferred_element_type=jnp.float32).astype(jnp.bfloat16)
+
+        @pl.when((lax.rem(j, 2) == 1) & (j >= 3) & (j < 3 + 2 * steps))
+        def _():
+            ring.step((j - 3) // 2)
+
+    for r in range(max(0, (count - 2) // 2), steps):
+        ring.step(jnp.int32(r))
+    ring.far_step(jnp.int32(0))
+    for delta in range(ring.len):
+        for c in range(2):
+            ring.wait_mate(delta, c)
+    out = pltpu.make_async_copy(buf, kv_ref, out_sem.at[0])
+    out.start()
+    ring.drain()
+    out.wait()
+
+
+def front(n, tokens, w_key, w_value, w_query, depth=4):
+    tok, hidden = tokens.shape
+    width = w_key.shape[1]
+    vmem = pl.BlockSpec(memory_space=pltpu.VMEM)
+    hbm = pl.BlockSpec(memory_space=pl.ANY)
+    dma = pltpu.SemaphoreType.DMA
+    weights = w_key.size + w_value.size + w_query.size
+    return pl.pallas_call(
+        functools.partial(front_body, n),
+        out_shape=(jax.ShapeDtypeStruct((tok, w_query.shape[1]), jnp.bfloat16),
+                   jax.ShapeDtypeStruct((n, 2, tok, width), jnp.bfloat16)),
+        in_specs=[vmem] + [hbm] * 3,
+        out_specs=(vmem, hbm),
+        scratch_shapes=[
+            pltpu.VMEM((n, 2, tok, width), jnp.bfloat16),
+            pltpu.VMEM((depth, hidden, width), jnp.bfloat16),
+            dma((depth,)), dma((1,)),
+        ] + ring_scratch(n, 2),
+        cost_estimate=pl.CostEstimate(flops=2 * tok * weights, bytes_accessed=2 * weights, transcendentals=0),
+        compiler_params=pltpu.CompilerParams(vmem_limit_bytes=40 * 2 ** 20, collective_id=1, has_side_effects=True),
+        name='front',
+    )(tokens, w_key, w_value, w_query)
+
+
 def tail_body(n, cap, o_ref, x_ref, rank_ref, router_ref, wo_ref, wg_ref, wu_ref, wd_ref, y_ref, e_ref,
-              buf, row_ref, act_ref, slots, table_out, table_in, sems, table_send, table_recv, *ring_sems):
+              buf, row_ref, act_ref, slots, stage, table_out, table_in, sems, stage_sem, table_send, table_recv, *ring_sems):
     f32, bf16 = jnp.float32, jnp.bfloat16
     ring = Ring(n, buf, *ring_sems)
     me = ring.me
@@ -297,25 +360,33 @@
     for i in range(1, n):
         table_arrival(i).wait_recv()
 
-    def expand(src, js):
+    def flush(slot, src):
+        return pltpu.make_async_copy(stage.at[slot], e_ref.at[:, pl.ds(pl.multiple_of(src * cap, cap), cap), :], stage_sem.at[slot])
+
+    def expand(slot, src, js):
         shape = (n_loc, cap, tok)
         table = table_in[src]
-        slot = lax.broadcasted_iota(jnp.int32, shape, 1).astype(f32)
-        sel = jnp.where(jnp.broadcast_to(table[:n_loc][:, None, :], shape) == slot, 1.0, 0.0)
+        place = lax.broadcasted_iota(jnp.int32, shape, 1).astype(f32)
+        sel = jnp.where(jnp.broadcast_to(table[:n_loc][:, None, :], shape) == place, 1.0, 0.0)
         scale = jnp.sum(sel * jnp.broadcast_to(table[n_loc:][:, None, :], shape), axis=2, keepdims=True).reshape(n_loc * cap, 1)
         sel = sel.reshape(n_loc * cap, tok).astype(bf16)
         for j in js:
             rows = jnp.dot(sel, buf[src, j], preferred_element_type=f32) * scale
-            e_ref[:, pl.ds(pl.multiple_of(src * cap, cap), cap), columns(j, width)] = rows.astype(bf16).reshape(n_loc, cap, width)
-
-    def expand_pair(delta):
-        expand(ring.owner(delta), range(chunks))
-
-        @pl.loop(0, chunks)
-        def _(j):
-            ring.wait_mate(delta, j)
-
-        expand(ring.owner(delta, ring.mate), range(chunks))
+            stage[slot, :, :, columns(j, width)] = rows.astype(bf16).reshape(n_loc, cap, width)
+
+    def expand_pair(delta, first):
+        for slot, base in ((0, me), (1, ring.mate)):
+            src = ring.owner(delta, base)
+            if slot == 1:
+                @pl.loop(0, chunks)
+                def _(j):
+                    ring.wait_mate(delta, j)
+
+            @pl.when(jnp.logical_not(first))
+            def _():
+                flush(slot, src).wait()
+            expand(slot, src, range(chunks))
+            flush(slot, src).start()
 
     done = 2 * chunks - LAG + chunks // 2
     length, far = n // 2, n // 4
@@ -327,7 +398,7 @@
 
         @pl.when(k < near)
         def _():
-            expand_pair(jnp.where(lax.rem(k, 2) == 1, length - (k + 1) // 2, k // 2))
+            expand_pair(jnp.where(lax.rem(k, 2) == 1, length - (k + 1) // 2, k // 2), k == 0)
 
     @pl.loop(0, chunks // 2)
     def _(i):
@@ -335,16 +406,24 @@
 
         @pl.when(i < 2)
         def _():
-            expand_pair(jnp.where(i == 0, far + 1, far - 1))
+            expand_pair(jnp.where(i == 0, far + 1, far - 1), i < 0)
+
+    ends = (ring.owner(far), ring.owner(far, ring.mate))
+    for slot in range(2):
+        flush(slot, ends[slot]).wait()
 
     @pl.loop(0, chunks // 2)
     def _(i):
         js = (i, i + chunks // 2)
-        expand(ring.owner(far), js)
+        expand(0, ends[0], js)
         for j in js:
             ring.wait_mate(far, j)
-        expand(ring.owner(far, ring.mate), js)
-
+        expand(1, ends[1], js)
+
+    for slot in range(2):
+        flush(slot, ends[slot]).start()
+    for slot in range(2):
+        flush(slot, ends[slot]).wait()
     ring.drain()
     for i in range(1, n):
         table_copy(i).wait_send()
@@ -363,18 +442,19 @@
         out_shape=(jax.ShapeDtypeStruct((tok, hidden), jnp.bfloat16),
                    jax.ShapeDtypeStruct((n_loc, n * cap, hidden), jnp.bfloat16)),
         in_specs=[vmem] * 4 + [hbm] * 4,
-        out_specs=(vmem, vmem),
+        out_specs=(vmem, hbm),
         scratch_shapes=[
             pltpu.VMEM((n, chunks, tok, width), jnp.bfloat16),
             pltpu.VMEM((tok, hidden), jnp.bfloat16),
             pltpu.VMEM((tok, hidden), jnp.bfloat16),
             pltpu.VMEM((depth, hidden, width), jnp.bfloat16),
+            pltpu.VMEM((2, n_loc, cap, hidden), jnp.bfloat16),
             pltpu.VMEM((n, 2 * n_loc, tok), jnp.float32),
             pltpu.VMEM((n, 2 * n_loc, tok), jnp.float32),
-            dma((depth,)), dma((n,)), dma((n,)),
+            dma((depth,)), dma((2,)), dma((n,)), dma((n,)),
         ] + ring_scratch(n, chunks),
         cost_estimate=pl.CostEstimate(flops=2 * tok * weights, bytes_accessed=2 * weights, transcendentals=0),
-        compiler_params=pltpu.CompilerParams(vmem_limit_bytes=67043328, collective_id=0, has_side_effects=True),
+        compiler_params=pltpu.CompilerParams(vmem_limit_bytes=44 * 2 ** 20, collective_id=0, has_side_effects=True),
         name='tail',
     )(attn, tokens, rank, w_router, w_out, w_gate, w_up, w_down)
 
@@ -393,16 +473,12 @@
     replicated = P()
 
     def local_step(tokens, w_query, w_key, w_value, w_out, w_gate, w_up, w_down, w_router, expert_ids):
-        f32, bf16 = jnp.float32, jnp.bfloat16
         tok = tokens.shape[0]
         n_grp = mesh.shape['sp']
         n_experts = w_router.shape[1]
         cap = max(2, (tok * expert_ids.shape[1] // n_experts) * 2)
         me = lax.axis_index('sp').astype(jnp.int32).reshape(1)
-        keys = jnp.dot(tokens, w_key, preferred_element_type=f32).astype(bf16)
-        values = jnp.dot(tokens, w_value, preferred_element_type=f32).astype(bf16)
-        kv_all = lax.all_gather(jnp.concatenate([keys, values], axis=1), 'sp', axis=0, tiled=True)
-        queries = jnp.dot(tokens, w_query, preferred_element_type=f32).astype(bf16)
+        queries, kv_all = front(n_grp, tokens, w_key, w_value, w_query)
         attn = attention(me, queries, kv_all)
         rank = slot_ranks(expert_ids, n_experts)
         hidden_out, expert_buf = tail(n_grp, cap, attn, tokens, rank, w_router, w_out, w_gate, w_up, w_down)

time: 245 us -> 197 us (0.80)
  matrix products: 28 us -> 0.21 us
  waiting for transfers between devices: 19.5 us -> 0 us
  between operations: 14.2 us -> 0.71 us
  Pallas kernels: 164 us -> 176 us
    pallas_call x0 -> x1, Pallas kernels: none -> 36 us  [front(): pl.pallas_call(functools.partial(front_body, n), out_shape=(jax.ShapeDtyp...]
    dot_general x3 -> x0, matrix products: 27.1 us -> none  [the longest x1 23 us: local_step(): queries = jnp.dot(tokens, w_query, preferred_element_type=f32).astype(bf16)]
    all_gather x1 -> x0, waiting for transfers between devices: 19.5 us -> none  [local_step(): lax.all_gather(jnp.concatenate([keys, values], axis=1), 'sp', axis=0, til...]
    pallas_call x1, Pallas kernels: 143 us -> 127 us  [tail(): pl.pallas_call(functools.partial(tail_body, n, cap), out_shape=(jax.Shape...]
    pallas_call x1, Pallas kernels: 21 us -> 13.1 us  [attention(): pl.pallas_call(functools.partial(attention_body, chunk, rows), out_shape=...]
  transfers between devices with their start and end apart: 1 -> 0, of which waited for: 1 -> 0; matrix products, arithmetic and copies ran while one was open for 10% -> 0% of each run, Pallas kernels for 0% -> 0%
where the time goes in v3:
time: 197 us
  Pallas kernels  176 us (89%)
  local copies, waits for them, and re-layouts  19.4 us (10%)
    pallas_call x1, Pallas kernels, tail(): pl.pallas_call(functools.partial(tail_body, n, cap), out_shape=(jax.Shape...  127 us
    pallas_call x1, Pallas kernels, front(): pl.pallas_call(functools.partial(front_body, n), out_shape=(jax.ShapeDtyp...  36 us
    unnamed x11, local copies, waits for them, and re-layouts  19.3 us
    pallas_call x1, Pallas kernels, attention(): pl.pallas_call(functools.partial(attention_body, chunk, rows), out_shape=...  13.1 us

profile of v3, /device:TPU:21, one launch (start us, length us, event | category | flops | bytes accessed | tf_op | source)
XLA Modules:
  0.0 196.9 jit_solution(641577510483563273)
XLA Ops:
  0.6 0.8 copy.13
  1.4 0.3 fusion
  1.7 0.1 copy.14
  1.8 0.2 convolution_select_fusion.rank_ref
  2.0 0.0 copy-start
  2.0 1.2 copy-done
  3.3 0.0 copy-start.2
  3.3 2.2 %copy-done.2 = bf16[4096,512]{1,0:T(8,128)(2,1)S(1)} copy-done((bf16[4096,512]{1,0:T(8,128)(2,1)S(1)}, bf16[4096,512]{1,0:T(8,128)(2,1)}, u32[]{:S(2)}) %copy-start.2) | copy-done | bytes 4194328
  5.5 36.0 %front.1 = (bf16[128,8192]{1,0:T(8,128)(2,1)S(1)}, bf16[16,2,128,512]{3,2,1,0:T(8,128)(2,1)S(1)}) custom-call(bf16[128,4096]{1,0:T(8,128)(2,1)S(1)} %copy-done, bf16[4096,512]{1,0:T(8,128)(2,1)S(1)} %copy-done.2, bf16[4096,512]{1,0:T(8,128)(2,1)} %wv_ref.1, bf16[4096,8192]{1,0:T(8,128)(2,1)} %wq_ref.1), custom_call_target="tpu_custom_call" | custom-call | flops 9663676416 | bytes 75497472 | tf_op jit(solution)/shard_map/front/pallas_call | solution.py:269
  41.4 0.0 copy-start.1
  41.4 0.0 copy-start.3
  41.5 13.1 %attention.1.o_ref = bf16[128,8192]{1,0:T(8,128)(2,1)S(1)} custom-call(s32[1]{0:T(128)} %bitcast.me_ref, bf16[128,8192]{1,0:T(8,128)(2,1)S(1)} %get-tuple-element.4.q_ref, bf16[16,2,128,512]{3,2,1,0:T(8,128)(2,1)S(1)} %get-tuple-element.5.k_ref.v_ref, bf16[16,2,128,512]{3,2,1,0:T(8,128)(2,1)S(1)} %get-tuple-element.5.k_ref.v_ref), custom_call_target="tpu_custom_call" | custom-call | flops 8589934592 | bytes 8388608 | tf_op jit(solution)/shard_map/attention/pallas_call | solution.py:68
  54.5 0.0 copy-done.1
  54.5 0.0 copy-done.3
  54.5 127.4 %tail.1 = (bf16[128,4096]{1,0:T(8,128)(2,1)S(1)}, bf16[8,256,4096]{2,1,0:T(8,128)(2,1)}) custom-call(bf16[128,8192]{1,0:T(8,128)(2,1)S(1)} %attention.1.o_ref, bf16[128,4096]{1,0:T(8,128)(2,1)S(1)} %copy-done.1, f32[128,128]{1,0:T(8,128)S(1)} %convolution_select_fusion.rank_ref, bf16[4096,128]{1,0:T(8,128)(2,1)S(1)} %copy-done.3, bf16[8192,4096]{1,0:T(8,128)(2,1)} %wo_ref.1, ...), custom_call_target="tpu_custom_call" | custom-call | flops 21474836480 | bytes 167772160 | tf_op jit(solution)/shard_map/tail/pallas_call | solution.py:440
  181.9 1.0 copy.18
  182.9 14.1 %copy.19 = bf16[8,256,4096]{2,1,0:T(8,128)(2,1)} copy(bf16[8,256,4096]{2,1,0:T(8,128)(2,1)} %get-tuple-element.9) | data formatting | bytes 33554432
  (1 shorter events, 0.0 us)
Async XLA Ops:
  2.0 1.2 copy-start
  3.3 2.2 %copy-start.2 = (bf16[4096,512]{1,0:T(8,128)(2,1)S(1)}, bf16[4096,512]{1,0:T(8,128)(2,1)}, u32[]{:S(2)}) copy-start(bf16[4096,512]{1,0:T(8,128)(2,1)} %wk_ref.1) | copy-start | bytes 12582916
  41.4 13.1 %copy-start.1 = (bf16[128,4096]{1,0:T(8,128)(2,1)S(1)}, bf16[128,4096]{1,0:T(8,128)(2,1)}, u32[]{:S(2)}) copy-start(bf16[128,4096]{1,0:T(8,128)(2,1)} %x_ref.3) | copy-start | bytes 3145732
  41.4 13.1 %copy-start.3 = (bf16[4096,128]{1,0:T(8,128)(2,1)S(1)}, bf16[4096,128]{1,0:T(8,128)(2,1)}, u32[]{:S(2)}) copy-start(bf16[4096,128]{1,0:T(8,128)(2,1)} %router_ref.1) | copy-start | bytes 3145732

commit v4 on v3

--- a/solution.py
+++ b/solution.py
@@ -28,25 +28,34 @@
     key = lax.broadcasted_iota(jnp.int32, bias_ref.shape, 1)
     bias_ref[...] = jnp.where(key <= pos, 0.0, -jnp.inf)
 
+    groups = heads // per
+    lanes = [slice(i * 128, (i + 1) * 128) for i in range(chunk // 128)]
+
     def step(c, masked):
         keys = k_ref[pl.ds(c * blocks, blocks), 0].reshape(chunk, HEAD_DIM)
         vals = v_ref[pl.ds(c * blocks, blocks), 0].reshape(chunk, HEAD_DIM)
-        for g in range(heads // per):
+
+        def score(g):
             q = jnp.concatenate([q_ref[:, (g * per + i) * HEAD_DIM:(g * per + i + 1) * HEAD_DIM] for i in range(per)], axis=0)
-            s = lax.dot_general(q, keys, NT, preferred_element_type=jnp.float32) * factor
+            return lax.dot_general(q, keys, NT, preferred_element_type=jnp.float32)
+
+        ahead = score(0)
+        for g in range(groups):
+            s = ahead
+            if g + 1 < groups:
+                ahead = score(g + 1)
+            s = [s[:, i] * factor for i in lanes]
             if masked:
-                s = (s.reshape(per, tok, chunk) + bias_ref[...][None]).reshape(rows, chunk)
+                s = [(x.reshape(per, tok, 128) + bias_ref[:, i][None]).reshape(rows, 128) for x, i in zip(s, lanes)]
             sl = pl.ds(g * rows, rows)
             m_old = m_ref[sl, :]
-            m_new = jnp.maximum(m_old, jnp.max(s, axis=1, keepdims=True))
-            p = jnp.exp2(s - m_new[:, :1])
+            m_new = jnp.maximum(m_old, jnp.max(functools.reduce(jnp.maximum, s), axis=1, keepdims=True))
+            p = [jnp.exp2(x - m_new) for x in s]
             alpha = jnp.exp2(m_old - m_new)
-            part = p[:, :128]
-            for i in range(1, chunk // 128):
-                part = part + p[:, i * 128:(i + 1) * 128]
-            l_ref[sl, :] = l_ref[sl, :] * alpha + part
-            acc_ref[sl, :] = acc_ref[sl, :] * alpha + jnp.dot(p.astype(jnp.bfloat16), vals, preferred_element_type=jnp.float32)
+            l_ref[sl, :] = l_ref[sl, :] * alpha + functools.reduce(jnp.add, p)
             m_ref[sl, :] = m_new
+            p = jnp.concatenate([x.astype(jnp.bfloat16) for x in p], axis=1)
+            acc_ref[sl, :] = acc_ref[sl, :] * alpha + jnp.dot(p, vals, preferred_element_type=jnp.float32)
 
     @pl.loop(0, full)
     def _(c):
@@ -67,7 +76,7 @@
     all_rows = tok * cols // HEAD_DIM
     return pl.pallas_call(
         functools.partial(attention_body, chunk, rows),
-        out_shape=jax.ShapeDtypeStruct((tok, width), jnp.bfloat16),
+        out_shape=pltpu.VMEM((tok, width), jnp.bfloat16),
         grid_spec=pltpu.PrefetchScalarGridSpec(
             num_scalar_prefetch=1,
             grid=(kv_heads,),
@@ -85,7 +94,7 @@
             ],
         ),
         cost_estimate=pl.CostEstimate(flops=4 * tok * width * n_src * tok, bytes_accessed=4 * tok * width + 2 * kv_all.size, transcendentals=0),
-        compiler_params=pltpu.CompilerParams(vmem_limit_bytes=40 * 2 ** 20),
+        compiler_params=pltpu.CompilerParams(vmem_limit_bytes=36 * 2 ** 20),
         name='attention',
     )(me, queries, kv_all, kv_all)
 
@@ -263,35 +272,36 @@
     tok, hidden = tokens.shape
     width = w_key.shape[1]
     vmem = pl.BlockSpec(memory_space=pltpu.VMEM)
-    hbm = pl.BlockSpec(memory_space=pl.ANY)
+    hbm = pl.BlockSpec(memory_space=pltpu.HBM)
     dma = pltpu.SemaphoreType.DMA
     weights = w_key.size + w_value.size + w_query.size
     return pl.pallas_call(
         functools.partial(front_body, n),
-        out_shape=(jax.ShapeDtypeStruct((tok, w_query.shape[1]), jnp.bfloat16),
-                   jax.ShapeDtypeStruct((n, 2, tok, width), jnp.bfloat16)),
+        out_shape=(pltpu.VMEM((tok, w_query.shape[1]), jnp.bfloat16),
+                   pltpu.VMEM((n, 2, tok, width), jnp.bfloat16)),
         in_specs=[vmem] + [hbm] * 3,
-        out_specs=(vmem, hbm),
+        out_specs=(vmem, vmem),
         scratch_shapes=[
             pltpu.VMEM((n, 2, tok, width), jnp.bfloat16),
             pltpu.VMEM((depth, hidden, width), jnp.bfloat16),
             dma((depth,)), dma((1,)),
         ] + ring_scratch(n, 2),
         cost_estimate=pl.CostEstimate(flops=2 * tok * weights, bytes_accessed=2 * weights, transcendentals=0),
-        compiler_params=pltpu.CompilerParams(vmem_limit_bytes=40 * 2 ** 20, collective_id=1, has_side_effects=True),
+        compiler_params=pltpu.CompilerParams(vmem_limit_bytes=52 * 2 ** 20, collective_id=1, has_side_effects=True),
         name='front',
     )(tokens, w_key, w_value, w_query)
 
 
-def tail_body(n, cap, o_ref, x_ref, rank_ref, router_ref, wo_ref, wg_ref, wu_ref, wd_ref, y_ref, e_ref,
-              buf, row_ref, act_ref, slots, stage, table_out, table_in, sems, stage_sem, table_send, table_recv, *ring_sems):
+def tail_body(n, cap, o_ref, x_ref, ids_ref, router_ref, wo_ref, wg_ref, wu_ref, wd_ref, y_ref, e_ref,
+              buf, row_ref, act_ref, slots, table_out, table_in, sems, table_send, table_recv, *ring_sems):
     f32, bf16 = jnp.float32, jnp.bfloat16
     ring = Ring(n, buf, *ring_sems)
     me = ring.me
     chunks, tok, width = buf.shape[1:]
     depth = slots.shape[1]
     parts = o_ref.shape[1] // depth
-    n_loc = rank_ref.shape[0] // n
+    n_exp = router_ref.shape[1]
+    n_loc = n_exp // n
     tiles = Tiles(slots, sems, (
         (parts * chunks, lambda t: [(None, wo_ref.at[columns(lax.rem(t, parts), depth), columns(t // parts, width)])]),
         ((parts + 2) * chunks, lambda t: [(lax.rem(t, 2) == 0, wg_ref.at[:, columns(t // 2, width)]),
@@ -317,9 +327,14 @@
         def _():
             ring.step(j - LAG)
 
+    expert = lax.broadcasted_iota(jnp.int32, (n_exp, tok), 0)
+    chosen = functools.reduce(jnp.logical_or, [ids_ref[c:c + 1, :] == expert for c in range(ids_ref.shape[0])])
+    earlier = lax.broadcasted_iota(jnp.int32, (tok, tok), 0) < lax.broadcasted_iota(jnp.int32, (tok, tok), 1)
+    count = jnp.dot(jnp.where(chosen, 1.0, 0.0).astype(bf16), jnp.where(earlier, 1.0, 0.0).astype(bf16), preferred_element_type=f32)
+    rank = jnp.where(chosen, count, -1.0)
     gate = jax.nn.sigmoid(jnp.dot(row_ref[...], router_ref[...], preferred_element_type=f32)).T
     for d in range(n):
-        table_out[d, :n_loc] = rank_ref[d * n_loc:(d + 1) * n_loc]
+        table_out[d, :n_loc] = rank[d * n_loc:(d + 1) * n_loc]
         table_out[d, n_loc:] = gate[d * n_loc:(d + 1) * n_loc]
     table_in[me] = table_out[me]
 
@@ -360,10 +375,7 @@
     for i in range(1, n):
         table_arrival(i).wait_recv()
 
-    def flush(slot, src):
-        return pltpu.make_async_copy(stage.at[slot], e_ref.at[:, pl.ds(pl.multiple_of(src * cap, cap), cap), :], stage_sem.at[slot])
-
-    def expand(slot, src, js):
+    def expand(src, js):
         shape = (n_loc, cap, tok)
         table = table_in[src]
         place = lax.broadcasted_iota(jnp.int32, shape, 1).astype(f32)
@@ -372,21 +384,16 @@
         sel = sel.reshape(n_loc * cap, tok).astype(bf16)
         for j in js:
             rows = jnp.dot(sel, buf[src, j], preferred_element_type=f32) * scale
-            stage[slot, :, :, columns(j, width)] = rows.astype(bf16).reshape(n_loc, cap, width)
-
-    def expand_pair(delta, first):
-        for slot, base in ((0, me), (1, ring.mate)):
-            src = ring.owner(delta, base)
-            if slot == 1:
-                @pl.loop(0, chunks)
-                def _(j):
-                    ring.wait_mate(delta, j)
-
-            @pl.when(jnp.logical_not(first))
-            def _():
-                flush(slot, src).wait()
-            expand(slot, src, range(chunks))
-            flush(slot, src).start()
+            e_ref[:, pl.ds(pl.multiple_of(src * cap, cap), cap), columns(j, width)] = rows.astype(bf16).reshape(n_loc, cap, width)
+
+    def expand_pair(delta):
+        expand(ring.owner(delta), range(chunks))
+
+        @pl.loop(0, chunks)
+        def _(j):
+            ring.wait_mate(delta, j)
+
+        expand(ring.owner(delta, ring.mate), range(chunks))
 
     done = 2 * chunks - LAG + chunks // 2
     length, far = n // 2, n // 4
@@ -398,73 +405,57 @@
 
         @pl.when(k < near)
         def _():
-            expand_pair(jnp.where(lax.rem(k, 2) == 1, length - (k + 1) // 2, k // 2), k == 0)
-
-    @pl.loop(0, chunks // 2)
-    def _(i):
-        ring.far_step(i)
-
-        @pl.when(i < 2)
-        def _():
-            expand_pair(jnp.where(i == 0, far + 1, far - 1), i < 0)
-
-    ends = (ring.owner(far), ring.owner(far, ring.mate))
-    for slot in range(2):
-        flush(slot, ends[slot]).wait()
-
-    @pl.loop(0, chunks // 2)
-    def _(i):
+            expand_pair(jnp.where(lax.rem(k, 2) == 1, length - (k + 1) // 2, k // 2))
+
+    def expand_far(i):
         js = (i, i + chunks // 2)
-        expand(0, ends[0], js)
+        expand(ring.owner(far), js)
         for j in js:
             ring.wait_mate(far, j)
-        expand(1, ends[1], js)
-
-    for slot in range(2):
-        flush(slot, ends[slot]).start()
-    for slot in range(2):
-        flush(slot, ends[slot]).wait()
+        expand(ring.owner(far, ring.mate), js)
+
+    half = chunks // 2
+    for i in range(half):
+        ring.far_step(jnp.int32(i))
+        if i < 2:
+            expand_pair(jnp.int32(far + 1 - 2 * i))
+
+    @pl.loop(0, half)
+    def _(i):
+        expand_far(i)
+
     ring.drain()
     for i in range(1, n):
         table_copy(i).wait_send()
 
 
-def tail(n, cap, attn, tokens, rank, w_router, w_out, w_gate, w_up, w_down, chunks=8, depth=4):
+def tail(n, cap, attn, tokens, ids, w_router, w_out, w_gate, w_up, w_down, chunks=8, depth=3):
     tok, hidden = tokens.shape
     width = hidden // chunks
-    n_loc = rank.shape[0] // n
+    n_loc = w_router.shape[1] // n
     vmem = pl.BlockSpec(memory_space=pltpu.VMEM)
-    hbm = pl.BlockSpec(memory_space=pl.ANY)
+    hbm = pl.BlockSpec(memory_space=pltpu.HBM)
     dma = pltpu.SemaphoreType.DMA
     weights = w_out.size + w_gate.size + w_up.size + w_down.size
     return pl.pallas_call(
         functools.partial(tail_body, n, cap),
-        out_shape=(jax.ShapeDtypeStruct((tok, hidden), jnp.bfloat16),
-                   jax.ShapeDtypeStruct((n_loc, n * cap, hidden), jnp.bfloat16)),
+        out_shape=(pltpu.VMEM((tok, hidden), jnp.bfloat16),
+                   pltpu.VMEM((n_loc, n * cap, hidden), jnp.bfloat16)),
         in_specs=[vmem] * 4 + [hbm] * 4,
-        out_specs=(vmem, hbm),
+        out_specs=(vmem, vmem),
         scratch_shapes=[
             pltpu.VMEM((n, chunks, tok, width), jnp.bfloat16),
             pltpu.VMEM((tok, hidden), jnp.bfloat16),
             pltpu.VMEM((tok, hidden), jnp.bfloat16),
             pltpu.VMEM((depth, hidden, width), jnp.bfloat16),
-            pltpu.VMEM((2, n_loc, cap, hidden), jnp.bfloat16),
             pltpu.VMEM((n, 2 * n_loc, tok), jnp.float32),
             pltpu.VMEM((n, 2 * n_loc, tok), jnp.float32),
-            dma((depth,)), dma((2,)), dma((n,)), dma((n,)),
+            dma((depth,)), dma((n,)), dma((n,)),
         ] + ring_scratch(n, chunks),
         cost_estimate=pl.CostEstimate(flops=2 * tok * weights, bytes_accessed=2 * weights, transcendentals=0),
-        compiler_params=pltpu.CompilerParams(vmem_limit_bytes=44 * 2 ** 20, collective_id=0, has_side_effects=True),
+        compiler_params=pltpu.CompilerParams(vmem_limit_bytes=41 * 2 ** 20, collective_id=0, has_side_effects=True),
         name='tail',
-    )(attn, tokens, rank, w_router, w_out, w_gate, w_up, w_down)
-
-
-def slot_ranks(expert_ids, n_experts):
-    tok = expert_ids.shape[0]
-    chosen = jnp.any(expert_ids[:, :, None] == jnp.arange(n_experts, dtype=jnp.int32), axis=1)
-    earlier = jnp.tril(jnp.ones((tok, tok), jnp.bfloat16), -1)
-    rank = jnp.dot(earlier, chosen.astype(jnp.bfloat16), preferred_element_type=jnp.float32)
-    return jnp.where(chosen, rank, -1.0).T
+    )(attn, tokens, ids, w_router, w_out, w_gate, w_up, w_down)
 
 
 def solution(mesh):
@@ -479,9 +470,8 @@
         cap = max(2, (tok * expert_ids.shape[1] // n_experts) * 2)
         me = lax.axis_index('sp').astype(jnp.int32).reshape(1)
         queries, kv_all = front(n_grp, tokens, w_key, w_value, w_query)
-        attn = attention(me, queries, kv_all)
-        rank = slot_ranks(expert_ids, n_experts)
-        hidden_out, expert_buf = tail(n_grp, cap, attn, tokens, rank, w_router, w_out, w_gate, w_up, w_down)
+        attn = pltpu.with_memory_space_constraint(attention(me, queries, kv_all), pltpu.VMEM)
+        hidden_out, expert_buf = tail(n_grp, cap, attn, tokens, expert_ids.T, w_router, w_out, w_gate, w_up, w_down)
         return hidden_out, expert_buf
 
     return jax.shard_map(local_step, mesh=mesh, in_specs=(row_spec,) + (replicated,) * 8 + (row_spec,), out_specs=(row_spec, buf_spec), check_vma=False)

time: 197 us -> 170 us (0.86)
  Pallas kernels: 176 us -> 162 us
  local copies, waits for them, and re-layouts: 19.4 us -> 7.13 us
    unnamed x11 -> x2, local copies, waits for them, and re-layouts: 19.3 us -> 7.13 us
    pallas_call x2, Pallas kernels: 163 us -> 153 us  [the longest x1 116 us: tail(): pl.pallas_call(functools.partial(tail_body, n, cap), out_shape=(pltpu.VME...]
    pallas_call x1, Pallas kernels: 13.1 us -> 8.95 us  [attention(): pl.pallas_call(functools.partial(attention_body, chunk, rows), out_shape=...]
where the time goes in v4:
time: 170 us; the launch traced here: 169 us
  Pallas kernels  162 us (95%)
  local copies, waits for them, and re-layouts  7.13 us (4%)
    pallas_call x1, Pallas kernels, tail(): pl.pallas_call(functools.partial(tail_body, n, cap), out_shape=(pltpu.VME...  116 us
    pallas_call x1, Pallas kernels, front(): pl.pallas_call(functools.partial(front_body, n), out_shape=(pltpu.VMEM((t...  36.7 us
    pallas_call x1, Pallas kernels, attention(): pl.pallas_call(functools.partial(attention_body, chunk, rows), out_shape=...  8.95 us
    unnamed x2, local copies, waits for them, and re-layouts  7.13 us

profile of v4, /device:TPU:21, one launch (start us, length us, event | category | flops | bytes accessed | tf_op | source)
XLA Modules:
  0.0 169.4 jit_solution(3612668139385944187)
XLA Ops:
  0.6 36.7 %front.1 = (bf16[128,8192]{1,0:T(8,128)(2,1)S(1)}, bf16[16,2,128,512]{3,2,1,0:T(8,128)(2,1)S(1)}) custom-call(bf16[128,4096]{1,0:T(8,128)(2,1)} %x_ref.3, bf16[4096,512]{1,0:T(8,128)(2,1)} %wk_ref.1, bf16[4096,512]{1,0:T(8,128)(2,1)} %wv_ref.1, bf16[4096,8192]{1,0:T(8,128)(2,1)} %wq_ref.1), custom_call_target="tpu_custom_call" | custom-call | flops 9663676416 | bytes 75497472 | tf_op jit(solution)/shard_map/front/pallas_call | solution.py:278
  37.4 8.9 %attention.1.o_ref = bf16[128,8192]{1,0:T(8,128)(2,1)S(1)} custom-call(s32[1]{0:T(128)} %bitcast.me_ref, bf16[128,8192]{1,0:T(8,128)(2,1)S(1)} %get-tuple-element.4.q_ref, bf16[16,2,128,512]{3,2,1,0:T(8,128)(2,1)S(1)} %get-tuple-element.5.k_ref.v_ref, bf16[16,2,128,512]{3,2,1,0:T(8,128)(2,1)S(1)} %get-tuple-element.5.k_ref.v_ref), custom_call_target="tpu_custom_call" | custom-call | flops 8589934592 | bytes 8388608 | tf_op jit(solution)/shard_map/attention/pallas_call | solution.py:77
  46.3 115.9 %tail.1 = (bf16[128,4096]{1,0:T(8,128)(2,1)S(1)}, bf16[8,256,4096]{2,1,0:T(8,128)(2,1)S(1)}) custom-call(bf16[128,8192]{1,0:T(8,128)(2,1)S(1)} %attention.1.o_ref, bf16[128,4096]{1,0:T(8,128)(2,1)} %x_ref.3, s32[8,128]{1,0:T(8,128)} %bitcast.2, bf16[4096,128]{1,0:T(8,128)(2,1)} %router_ref.1, bf16[8192,4096]{1,0:T(8,128)(2,1)} %wo_ref.1, ...), custom_call_target="tpu_custom_call" | custom-call | flops 21474836480 | bytes 167772160 | tf_op jit(solution)/shard_map/tail/pallas_call | solution.py:440
  162.3 1.0 copy.14
  163.2 6.2 %copy.15 = bf16[8,256,4096]{2,1,0:T(8,128)(2,1)} copy(bf16[8,256,4096]{2,1,0:T(8,128)(2,1)S(1)} %get-tuple-element.7) | data formatting | bytes 33554432

commit v5 on v2

v5 whole, which is shorter than its diff:
```python
import functools
import math
import jax
import jax.numpy as jnp
from jax import lax
from jax.experimental import pallas as pl
from jax.experimental.pallas import tpu as pltpu
from jax.sharding import PartitionSpec as P

HEAD_DIM = 128
NT = (((1,), (1,)), ((), ()))
MESH = pl.DeviceIdType.MESH


class Ring:
    def __init__(self, n, piece, up_send, down_send, ring_recv, mate_send, mate_recv):
        self.n, self.len, self.chunks = n, n // 2, up_send.shape[1]
        self.half = self.chunks // 2
        self.piece, self.up_send, self.down_send = piece, up_send, down_send
        self.ring_recv, self.mate_send, self.mate_recv = ring_recv, mate_send, mate_recv
        self.me = lax.axis_index('sp')
        self.mate = self.me + 1 - 2 * lax.rem(self.me, 2)
        self.up = lax.rem(self.me + 2, n)
        self.down = lax.rem(self.me + n - 2, n)

    def barrier(self):
        sem = pltpu.get_barrier_semaphore()
        for i in range(1, self.n):
            pl.semaphore_signal(sem, inc=1, device_id={'sp': lax.rem(self.me + i, self.n)}, device_id_type=MESH)
        pl.semaphore_wait(sem, self.n - 1)

    def owner(self, delta, base=None):
        return lax.rem((self.me if base is None else base) + 2 * delta, self.n)

    def copy(self, delta, j, send_sem, recv_sem, target):
        piece = self.piece(self.owner(delta), j)
        return pltpu.make_async_remote_copy(src_ref=piece, dst_ref=piece, send_sem=send_sem, recv_sem=recv_sem,
                                            device_id={'sp': target}, device_id_type=MESH)

    def up_copy(self, dist, j):
        delta = lax.rem(self.len - dist, self.len)
        return self.copy(delta, j, self.up_send.at[dist, j], self.ring_recv.at[lax.rem(delta + self.len - 1, self.len), j], self.up)

    def down_copy(self, dist, j):
        return self.copy(dist, j, self.down_send.at[dist, j], self.ring_recv.at[dist + 1, j], self.down)

    def mate_copy(self, delta, j):
        return self.copy(delta, j, self.mate_send.at[delta, j], self.mate_recv.at[delta, j], self.mate)

    def wait_ring(self, delta, j):
        self.copy(delta, j, self.mate_send.at[delta, j], self.ring_recv.at[delta, j], self.mate).wait_recv()

    def wait_mate(self, delta, j):
        piece = self.piece(self.owner(delta, self.mate), j)
        pltpu.make_async_remote_copy(src_ref=piece, dst_ref=piece, send_sem=self.mate_send.at[delta, j], recv_sem=self.mate_recv.at[delta, j],
                                     device_id={'sp': self.mate}, device_id_type=MESH).wait_recv()

    def send_own(self, j):
        self.up_copy(0, j).start()
        self.down_copy(0, j).start()
        self.mate_copy(0, j).start()

    def step(self, r):
        dist, j = r // self.chunks + 1, lax.rem(r, self.chunks)
        last = 2 * self.chunks
        self.wait_ring(self.len - dist, j)

        @pl.when(r < last + self.half)
        def _():
            self.up_copy(dist, j).start()

        self.mate_copy(self.len - dist, j).start()
        self.wait_ring(dist, j)

        @pl.when((r < last) | (r >= last + self.half))
        def _():
            self.down_copy(dist, j).start()

        self.mate_copy(dist, j).start()

    def far_step(self, i):
        far = self.len // 2
        for j in (i, i + self.half):
            self.wait_ring(far, j)
            self.mate_copy(far, j).start()

    def drain(self):
        far = self.len // 2

        @pl.loop(0, self.chunks)
        def _(j):
            for dist in range(far):
                @pl.when((dist < far - 1) | (j < self.half))
                def _(dist=dist):
                    self.up_copy(dist, j).wait_send()

                @pl.when((dist < far - 1) | (j >= self.half))
                def _(dist=dist):
                    self.down_copy(dist, j).wait_send()
            for delta in range(self.len):
                self.mate_copy(delta, j).wait_send()


def ring_scratch(n, chunks):
    length, far = n // 2, n // 4
    dma = pltpu.SemaphoreType.DMA
    return [dma((far, chunks)), dma((far, chunks)), dma((length, chunks)), dma((length, chunks)), dma((length, chunks))]


class Tiles:
    def __init__(self, slots, sems, groups):
        self.slots, self.sems, self.groups = slots, sems, groups
        self.depth, self.total = slots.shape[0], groups[-1][0]

    def copy(self, tile, slot):
        return pltpu.make_async_copy(tile, self.slots.at[slot], self.sems.at[slot])

    def start(self, t):
        first = 0
        for end, pick in self.groups:
            @pl.when((t >= first) & (t < end))
            def _(first=first, pick=pick):
                for cond, tile in pick(t - first):
                    if cond is None:
                        self.copy(tile, lax.rem(t, self.depth)).start()
                    else:
                        @pl.when(cond)
                        def _(tile=tile):
                            self.copy(tile, lax.rem(t, self.depth)).start()
            first = end

    def prime(self):
        for t in range(self.depth - 1):
            self.start(jnp.int32(t))

    def take(self, t):
        self.start(t + self.depth - 1)
        slot = lax.rem(t, self.depth)
        self.copy(self.groups[0][1](0)[0][1], slot).wait()
        return self.slots.at[slot]


def columns(j, width):
    return pl.ds(pl.multiple_of(j * width, width), width)


def block_body(n, cap, span, rows, x_ref, ids_ref, wk_ref, wv_ref, wq_ref, wr_ref, wo_ref, wg_ref, wu_ref, wd_ref, y_ref, e_ref,
               buf, q_ref, row_ref, slots, router_ref, m_ref, l_ref, acc_ref, bias_ref, table_out, table_in,
               sems, router_sem, table_send, table_recv, *ring_sems):
    f32, bf16 = jnp.float32, jnp.bfloat16
    chunks, tok, width = buf.shape[1:]
    depth = slots.shape[1]
    n_exp = router_ref.shape[1]
    n_loc = n_exp // n
    kv_heads = width // HEAD_DIM
    q_tiles = q_ref.shape[1] // width
    parts = q_ref.shape[1] // depth
    act_ref = q_ref.at[:, :depth]

    def kv_piece(src, j):
        return e_ref.at[lax.rem(src, n_loc), columns(src // n_loc, tok), columns(j, width)]

    kv_ring = Ring(n, kv_piece, *ring_sems[:5])
    ring = Ring(n, lambda src, j: buf.at[src, j], *ring_sems[5:])
    me = ring.me
    ends = [1, 2, 2 + q_tiles, 2 + q_tiles + parts * chunks, 2 + q_tiles + (parts + 2) * chunks, 2 + q_tiles + (parts + 3) * chunks]
    tiles = Tiles(slots, sems, (
        (ends[0], lambda t: [(None, wk_ref)]),
        (ends[1], lambda t: [(None, wv_ref)]),
        (ends[2], lambda t: [(None, wq_ref.at[:, columns(t, width)])]),
        (ends[3], lambda t: [(None, wo_ref.at[columns(lax.rem(t, parts), depth), columns(t // parts, width)])]),
        (ends[4], lambda t: [(lax.rem(t, 2) == 0, wg_ref.at[:, columns(t // 2, width)]),
                             (lax.rem(t, 2) == 1, wu_ref.at[:, columns(t // 2, width)])]),
        (ends[5], lambda t: [(None, wd_ref.at[:, columns(t, width)])]),
    ))
    tiles.prime()
    router_copy = pltpu.make_async_copy(wr_ref, router_ref, router_sem.at[0])
    router_copy.start()
    ring.barrier()

    for c in range(2):
        part = jnp.dot(x_ref[...], tiles.take(jnp.int32(c))[...], preferred_element_type=f32).astype(bf16)
        e_ref[lax.rem(me, n_loc), columns(me // n_loc, tok), c * width:(c + 1) * width] = part
        kv_ring.send_own(jnp.int32(c))

    kv_steps = 3 * kv_ring.chunks

    @pl.loop(0, q_tiles)
    def _(j):
        q_ref[:, columns(j, width)] = jnp.dot(x_ref[...], tiles.take(j + 2)[...], preferred_element_type=f32).astype(bf16)

        @pl.when((lax.rem(j, 2) == 1) & (j >= 3) & (j < 3 + 2 * kv_steps))
        def _():
            kv_ring.step((j - 3) // 2)

    for r in range((q_tiles - 2) // 2, kv_steps):
        kv_ring.step(jnp.int32(r))
    kv_ring.far_step(jnp.int32(0))
    for delta in range(kv_ring.len):
        for c in range(2):
            kv_ring.wait_mate(delta, c)

    per = rows // tok
    heads = q_ref.shape[1] // (kv_heads * HEAD_DIM)
    groups = heads // per
    blocks = span // tok
    halves = n_loc // blocks
    factor = math.log2(math.e) / math.sqrt(HEAD_DIM)
    full = (me * tok) // span
    lanes = [slice(i * 128, (i + 1) * 128) for i in range(span // 128)]
    pos = me * tok - full * span + lax.broadcasted_iota(jnp.int32, bias_ref.shape, 0)
    bias_ref[...] = jnp.where(lax.broadcasted_iota(jnp.int32, bias_ref.shape, 1) <= pos, 0.0, -jnp.inf)

    def head_columns(i, h):
        return columns(i * heads + h, HEAD_DIM)

    def key_block(c, col):
        return e_ref[pl.ds(lax.rem(c, halves) * blocks, blocks), columns(c // halves, tok), columns(col, HEAD_DIM)].reshape(span, HEAD_DIM)

    def attend(i, c, first):
        keys = key_block(c, i)
        vals = key_block(c, kv_heads + i)

        def score(g):
            q = jnp.concatenate([q_ref[:, head_columns(i, g * per + h)] for h in range(per)], axis=0)
            return lax.dot_general(q, keys, NT, preferred_element_type=f32)

        ahead = score(0)
        for g in range(groups):
            s = ahead
            if g + 1 < groups:
                ahead = score(g + 1)
            s = [s[:, k] * factor for k in lanes]
            sl = pl.ds(g * rows, rows)
            if first:
                s = [(x.reshape(per, tok, 128) + bias_ref[:, k][None]).reshape(rows, 128) for x, k in zip(s, lanes)]
            m_new = jnp.max(functools.reduce(jnp.maximum, s), axis=1, keepdims=True)
            if first:
                m_new = jnp.broadcast_to(m_new, (rows, 128))
            else:
                m_old = m_ref[sl, :]
                m_new = jnp.maximum(m_old, m_new)
                alpha = jnp.exp2(m_old - m_new)
            m_ref[sl, :] = m_new
            p = [jnp.exp2(x - m_new) for x in s]
            total = functools.reduce(jnp.add, p)
            out = jnp.dot(jnp.concatenate([x.astype(bf16) for x in p], axis=1), vals, preferred_element_type=f32)
            l_ref[sl, :] = total if first else l_ref[sl, :] * alpha + total
            acc_ref[sl, :] = out if first else acc_ref[sl, :] * alpha + out

    @pl.loop(0, kv_heads)
    def _(i):
        attend(i, full, True)

        @pl.loop(0, full)
        def _(c):
            attend(i, c, False)

        for h in range(heads):
            sl = pl.ds(h * tok, tok)
            total = jnp.sum(l_ref[sl, :], axis=1, keepdims=True)
            q_ref[:, head_columns(i, h)] = (acc_ref[sl, :] * (1.0 / total)).astype(bf16)

    @pl.loop(0, chunks)
    def _(j):
        part = None
        for i in range(parts):
            prod = jnp.dot(q_ref[:, i * depth:(i + 1) * depth], tiles.take(ends[2] + parts * j + i)[...], preferred_element_type=f32)
            part = prod if part is None else part + prod
        h = (x_ref[:, columns(j, width)].astype(f32) + part).astype(bf16)
        buf[me, j] = h
        row_ref[:, columns(j, width)] = h
        ring.send_own(j)

    router_copy.wait()
    expert = lax.broadcasted_iota(jnp.int32, (n_exp, tok), 0)
    chosen = functools.reduce(jnp.logical_or, [ids_ref[c:c + 1, :] == expert for c in range(ids_ref.shape[0])])
    earlier = lax.broadcasted_iota(jnp.int32, (tok, tok), 0) < lax.broadcasted_iota(jnp.int32, (tok, tok), 1)
    count = jnp.dot(jnp.where(chosen, 1.0, 0.0).astype(bf16), jnp.where(earlier, 1.0, 0.0).astype(bf16), preferred_element_type=f32)
    rank = jnp.where(chosen, count, -1.0)
    gate = jax.nn.sigmoid(jnp.dot(row_ref[...], router_ref[...], preferred_element_type=f32)).T
    for d in range(n):
        table_out[d, :n_loc] = rank[d * n_loc:(d + 1) * n_loc]
        table_out[d, n_loc:] = gate[d * n_loc:(d + 1) * n_loc]
    table_in[me] = table_out[me]

    def table_copy(i):
        dst = lax.rem(me + i, n)
        return pltpu.make_async_remote_copy(src_ref=table_out.at[dst], dst_ref=table_in.at[me], send_sem=table_send.at[i], recv_sem=table_recv.at[i],
                                            device_id={'sp': dst}, device_id_type=MESH)

    def table_arrival(i):
        src = lax.rem(me + n - i, n)
        return pltpu.make_async_remote_copy(src_ref=table_out.at[src], dst_ref=table_in.at[src], send_sem=table_send.at[i], recv_sem=table_recv.at[i],
                                            device_id={'sp': src}, device_id_type=MESH)

    for i in range(1, n):
        table_copy(i).start()

    half = chunks // 2

    @pl.loop(0, chunks)
    def _(j):
        h = row_ref[...]
        g = jnp.dot(h, tiles.take(ends[3] + 2 * j)[...], preferred_element_type=f32)
        u = jnp.dot(h, tiles.take(ends[3] + 2 * j + 1)[...], preferred_element_type=f32)
        act_ref[:, columns(j, width)] = (g * jax.nn.sigmoid(g) * u).astype(bf16)
        ring.step(j + jnp.minimum(j, half))

        @pl.when(j < half)
        def _():
            ring.step(2 * j + 1)

    @pl.loop(0, chunks)
    def _(j):
        y = jnp.dot(act_ref[...], tiles.take(ends[4] + j)[...], preferred_element_type=f32)
        y_ref[:, columns(j, width)] = (row_ref[:, columns(j, width)].astype(f32) + y).astype(bf16)

        @pl.when(lax.rem(j, 2) == 1)
        def _():
            ring.step(chunks + half + j // 2)

    kv_ring.drain()
    for i in range(1, n):
        table_arrival(i).wait_recv()

    def expand(src, js):
        shape = (n_loc, cap, tok)
        table = table_in[src]
        place = lax.broadcasted_iota(jnp.int32, shape, 1).astype(f32)
        sel = jnp.where(jnp.broadcast_to(table[:n_loc][:, None, :], shape) == place, 1.0, 0.0)
        scale = jnp.sum(sel * jnp.broadcast_to(table[n_loc:][:, None, :], shape), axis=2, keepdims=True).reshape(n_loc * cap, 1)
        sel = sel.reshape(n_loc * cap, tok).astype(bf16)
        for j in js:
            out = jnp.dot(sel, buf[src, j], preferred_element_type=f32) * scale
            e_ref[:, pl.ds(pl.multiple_of(src * cap, cap), cap), columns(j, width)] = out.astype(bf16).reshape(n_loc, cap, width)

    def expand_pair(delta):
        expand(ring.owner(delta), range(chunks))

        @pl.loop(0, chunks)
        def _(j):
            ring.wait_mate(delta, j)

        expand(ring.owner(delta, ring.mate), range(chunks))

    length, far = n // 2, n // 4
    near = 2 * far - 3

    @pl.loop(0, chunks)
    def _(k):
        ring.step(2 * chunks + k)

        @pl.when(k < near)
        def _():
            expand_pair(jnp.where(lax.rem(k, 2) == 1, length - (k + 1) // 2, k // 2))

    def expand_far(i):
        js = (i, i + half)
        expand(ring.owner(far), js)
        for j in js:
            ring.wait_mate(far, j)
        expand(ring.owner(far, ring.mate), js)

    @pl.loop(0, half)
    def _(i):
        ring.far_step(i)

        @pl.when(i < 2)
        def _():
            expand_pair(far + 1 - 2 * i)

        @pl.when(i > 0)
        def _():
            expand_far(i - 1)

    expand_far(jnp.int32(half - 1))
    ring.drain()
    for i in range(1, n):
        table_copy(i).wait_send()


def moe_block(n, cap, tokens, ids, w_key, w_value, w_query, w_router, w_out, w_gate, w_up, w_down, depth=3, span=512, rows=512):
    tok, hidden = tokens.shape
    width = w_key.shape[1]
    q_width = w_query.shape[1]
    chunks = hidden // width
    n_exp = w_router.shape[1]
    n_loc = n_exp // n
    all_rows = tok * q_width // width
    vmem = pl.BlockSpec(memory_space=pltpu.VMEM)
    hbm = pl.BlockSpec(memory_space=pltpu.HBM)
    dma = pltpu.SemaphoreType.DMA
    weights = 2 * w_key.size + w_query.size + w_out.size + w_gate.size + w_up.size + w_down.size
    return pl.pallas_call(
        functools.partial(block_body, n, cap, span, rows),
        out_shape=(pltpu.VMEM((tok, hidden), jnp.bfloat16), pltpu.VMEM((n_loc, n * cap, hidden), jnp.bfloat16)),
        in_specs=[vmem] * 2 + [hbm] * 8,
        out_specs=(vmem, vmem),
        scratch_shapes=[
            pltpu.VMEM((n, chunks, tok, width), jnp.bfloat16),
            pltpu.VMEM((tok, q_width), jnp.bfloat16),
            pltpu.VMEM((tok, hidden), jnp.bfloat16),
            pltpu.VMEM((depth, hidden, width), jnp.bfloat16),
            pltpu.VMEM(w_router.shape, jnp.bfloat16),
            pltpu.VMEM((all_rows, 128), jnp.float32),
            pltpu.VMEM((all_rows, 128), jnp.float32),
            pltpu.VMEM((all_rows, 128), jnp.float32),
            pltpu.VMEM((tok, span), jnp.float32),
            pltpu.VMEM((n, 2 * n_loc, tok), jnp.float32),
            pltpu.VMEM((n, 2 * n_loc, tok), jnp.float32),
            dma((depth,)), dma((1,)), dma((n,)), dma((n,)),
        ] + ring_scratch(n, 2) + ring_scratch(n, chunks),
        cost_estimate=pl.CostEstimate(flops=2 * tok * weights, bytes_accessed=2 * weights, transcendentals=0),
        compiler_params=pltpu.CompilerParams(vmem_limit_bytes=45 * 2 ** 20, collective_id=0, has_side_effects=True),
        name='moe_block',
    )(tokens, ids, w_key, w_value, w_query, w_router, w_out, w_gate, w_up, w_down)


def solution(mesh):
    row_spec = P(('dp', 'sp'), None)
    buf_spec = P(('dp', 'sp'), None, None)
    replicated = P()

    def local_step(tokens, w_query, w_key, w_value, w_out, w_gate, w_up, w_down, w_router, expert_ids):
        tok = tokens.shape[0]
        n_grp = mesh.shape['sp']
        n_experts = w_router.shape[1]
        cap = max(2, (tok * expert_ids.shape[1] // n_experts) * 2)
        hidden_out, expert_buf = moe_block(n_grp, cap, tokens, expert_ids.T, w_key, w_value, w_query, w_router, w_out, w_gate, w_up, w_down)
        return hidden_out, expert_buf

    return jax.shard_map(local_step, mesh=mesh, in_specs=(row_spec,) + (replicated,) * 8 + (row_spec,), out_specs=(row_spec, buf_spec), check_vma=False)
```

time: 245 us -> 164 us (0.67)
  matrix products: 28 us -> 0 us
  waiting for transfers between devices: 19.5 us -> 0 us
  between operations: 14.2 us -> 0.64 us
  local copies, waits for them, and re-layouts: 18.5 us -> 7.13 us
  Pallas kernels: 164 us -> 156 us
    dot_general x4 -> x0, matrix products: 28 us -> none  [the longest x1 23 us: local_step(): queries = jnp.dot(tokens, w_query, preferred_element_type=f32).astype(bf16)]
    all_gather x1 -> x0, waiting for transfers between devices: 19.5 us -> none  [local_step(): lax.all_gather(jnp.concatenate([keys, values], axis=1), 'sp', axis=0, til...]
    unnamed x11 -> x2, local copies, waits for them, and re-layouts: 18.4 us -> 7.13 us
    pallas_call x2 -> x1, Pallas kernels: 164 us -> 156 us  [moe_block(): pl.pallas_call(functools.partial(block_body, n, cap, span, rows), out_sha...]
  transfers between devices with their start and end apart: 1 -> 0, of which waited for: 1 -> 0; matrix products, arithmetic and copies ran while one was open for 10% -> 0% of each run, Pallas kernels for 0% -> 0%
where the time goes in v5:
time: 164 us
  Pallas kernels  156 us (95%)
  local copies, waits for them, and re-layouts  7.13 us (4%)
    pallas_call x1, Pallas kernels, moe_block(): pl.pallas_call(functools.partial(block_body, n, cap, span, rows), out_sha...  156 us
    unnamed x2, local copies, waits for them, and re-layouts  7.13 us

profile of v5, /device:TPU:21, one launch (start us, length us, event | category | flops | bytes accessed | tf_op | source)
XLA Modules:
  0.0 164.2 jit_solution(3443081220188650310)
XLA Ops:
  0.6 156.4 %moe_block.1 = (bf16[128,4096]{1,0:T(8,128)(2,1)S(1)}, bf16[8,256,4096]{2,1,0:T(8,128)(2,1)S(1)}) custom-call(bf16[128,4096]{1,0:T(8,128)(2,1)} %x_ref.1, s32[8,128]{1,0:T(8,128)} %bitcast.1, bf16[4096,512]{1,0:T(8,128)(2,1)} %wk_ref.1, bf16[4096,512]{1,0:T(8,128)(2,1)} %wv_ref.1, bf16[4096,8192]{1,0:T(8,128)(2,1)} %wq_ref.1, bf16[4096,128]{1,0:T(8,128)(2,1)} %wr_ref.1, ...), custom_call_target="tpu_custom_call" | custom-call | flops 31138512896 | bytes 243269632 | tf_op jit(solution)/shard_map/moe_block/pallas_call | solution.py:395
  157.0 1.0 copy.14
  158.0 6.2 %copy.15 = bf16[8,256,4096]{2,1,0:T(8,128)(2,1)} copy(bf16[8,256,4096]{2,1,0:T(8,128)(2,1)S(1)} %get-tuple-element.3) | data formatting | bytes 33554432

commit v6 on v5

--- a/solution.py
+++ b/solution.py
@@ -195,10 +195,11 @@
 
     for r in range((q_tiles - 2) // 2, kv_steps):
         kv_ring.step(jnp.int32(r))
-    kv_ring.far_step(jnp.int32(0))
+    far = n // 4
     for delta in range(kv_ring.len):
-        for c in range(2):
-            kv_ring.wait_mate(delta, c)
+        if delta != far:
+            for c in range(2):
+                kv_ring.wait_mate(delta, c)
 
     per = rows // tok
     heads = q_ref.shape[1] // (kv_heads * HEAD_DIM)
@@ -248,13 +249,28 @@
             l_ref[sl, :] = total if first else l_ref[sl, :] * alpha + total
             acc_ref[sl, :] = out if first else acc_ref[sl, :] * alpha + out
 
+    last = jnp.maximum(full - 2 * far // blocks, 0)
+
+    def far_keys():
+        kv_ring.far_step(jnp.int32(0))
+        for c in range(2):
+            kv_ring.wait_mate(far, c)
+
     @pl.loop(0, kv_heads)
     def _(i):
         attend(i, full, True)
 
         @pl.loop(0, full)
-        def _(c):
-            attend(i, c, False)
+        def _(k):
+            @pl.when((i == 0) & (k == full - 1))
+            def _():
+                far_keys()
+
+            attend(i, jnp.where(k == full - 1, last, jnp.where(k < last, k, k + 1)), False)
+
+        @pl.when((i == 0) & (full == 0))
+        def _():
+            far_keys()
 
         for h in range(heads):
             sl = pl.ds(h * tok, tok)
@@ -344,7 +360,7 @@
 
         expand(ring.owner(delta, ring.mate), range(chunks))
 
-    length, far = n // 2, n // 4
+    length = n // 2
     near = 2 * far - 3
 
     @pl.loop(0, chunks)

time: 164 us -> 162 us (0.988)
  Pallas kernels: 156 us -> 154 us
    pallas_call x1, Pallas kernels: 156 us -> 154 us  [moe_block(): pl.pallas_call(functools.partial(block_body, n, cap, span, rows), out_sha...]
where the time goes in v6:
time: 162 us
  Pallas kernels  154 us (95%)
  local copies, waits for them, and re-layouts  7.13 us (4%)
    pallas_call x1, Pallas kernels, moe_block(): pl.pallas_call(functools.partial(block_body, n, cap, span, rows), out_sha...  154 us
    unnamed x2, local copies, waits for them, and re-layouts  7.13 us

profile of v6, /device:TPU:21, one launch (start us, length us, event | category | flops | bytes accessed | tf_op | source)
XLA Modules:
  0.0 161.7 jit_solution(4518392217396374213)
XLA Ops:
  0.6 153.9 %moe_block.1 = (bf16[128,4096]{1,0:T(8,128)(2,1)S(1)}, bf16[8,256,4096]{2,1,0:T(8,128)(2,1)S(1)}) custom-call(bf16[128,4096]{1,0:T(8,128)(2,1)} %x_ref.1, s32[8,128]{1,0:T(8,128)} %bitcast.1, bf16[4096,512]{1,0:T(8,128)(2,1)} %wk_ref.1, bf16[4096,512]{1,0:T(8,128)(2,1)} %wv_ref.1, bf16[4096,8192]{1,0:T(8,128)(2,1)} %wq_ref.1, bf16[4096,128]{1,0:T(8,128)(2,1)} %wr_ref.1, ...), custom_call_target="tpu_custom_call" | custom-call | flops 31138512896 | bytes 243269632 | tf_op jit(solution)/shard_map/moe_block/pallas_call | solution.py:411
  154.5 1.0 copy.14
  155.5 6.2 %copy.15 = bf16[8,256,4096]{2,1,0:T(8,128)(2,1)} copy(bf16[8,256,4096]{2,1,0:T(8,128)(2,1)S(1)} %get-tuple-element.3) | data formatting | bytes 33554432

commit v7 on v6

--- a/solution.py
+++ b/solution.py
@@ -146,14 +146,15 @@
 
 def block_body(n, cap, span, rows, x_ref, ids_ref, wk_ref, wv_ref, wq_ref, wr_ref, wo_ref, wg_ref, wu_ref, wd_ref, y_ref, e_ref,
                buf, q_ref, row_ref, slots, router_ref, m_ref, l_ref, acc_ref, bias_ref, table_out, table_in,
-               sems, router_sem, table_send, table_recv, *ring_sems):
+               x_mate_ref, sems, router_sem, table_send, table_recv, x_sem, q_send, q_recv, *ring_sems):
     f32, bf16 = jnp.float32, jnp.bfloat16
     chunks, tok, width = buf.shape[1:]
     depth = slots.shape[1]
     n_exp = router_ref.shape[1]
     n_loc = n_exp // n
     kv_heads = width // HEAD_DIM
-    q_tiles = q_ref.shape[1] // width
+    q_tiles = q_ref.shape[1] // (2 * width)
+    core = lax.rem(lax.axis_index('sp'), 2)
     parts = q_ref.shape[1] // depth
     act_ref = q_ref.at[:, :depth]
 
@@ -167,7 +168,7 @@
     tiles = Tiles(slots, sems, (
         (ends[0], lambda t: [(None, wk_ref)]),
         (ends[1], lambda t: [(None, wv_ref)]),
-        (ends[2], lambda t: [(None, wq_ref.at[:, columns(t, width)])]),
+        (ends[2], lambda t: [(None, wq_ref.at[:, columns(core * q_tiles + t, width)])]),
         (ends[3], lambda t: [(None, wo_ref.at[columns(lax.rem(t, parts), depth), columns(t // parts, width)])]),
         (ends[4], lambda t: [(lax.rem(t, 2) == 0, wg_ref.at[:, columns(t // 2, width)]),
                              (lax.rem(t, 2) == 1, wu_ref.at[:, columns(t // 2, width)])]),
@@ -177,6 +178,9 @@
     router_copy = pltpu.make_async_copy(wr_ref, router_ref, router_sem.at[0])
     router_copy.start()
     ring.barrier()
+    x_copy = pltpu.make_async_remote_copy(src_ref=x_ref, dst_ref=x_mate_ref, send_sem=x_sem.at[0], recv_sem=x_sem.at[1],
+                                          device_id={'sp': ring.mate}, device_id_type=MESH)
+    x_copy.start()
 
     for c in range(2):
         part = jnp.dot(x_ref[...], tiles.take(jnp.int32(c))[...], preferred_element_type=f32).astype(bf16)
@@ -185,21 +189,39 @@
 
     kv_steps = 3 * kv_ring.chunks
 
+    def q_copy(j, owner):
+        return pltpu.make_async_remote_copy(src_ref=row_ref.at[:, columns(j, width)], dst_ref=q_ref.at[:, columns(owner * q_tiles + j, width)],
+                                            send_sem=q_send.at[j], recv_sem=q_recv.at[j], device_id={'sp': ring.mate}, device_id_type=MESH)
+
+    x_copy.wait_recv()
+
     @pl.loop(0, q_tiles)
     def _(j):
-        q_ref[:, columns(j, width)] = jnp.dot(x_ref[...], tiles.take(j + 2)[...], preferred_element_type=f32).astype(bf16)
-
-        @pl.when((lax.rem(j, 2) == 1) & (j >= 3) & (j < 3 + 2 * kv_steps))
-        def _():
-            kv_ring.step((j - 3) // 2)
-
-    for r in range((q_tiles - 2) // 2, kv_steps):
-        kv_ring.step(jnp.int32(r))
+        tile = tiles.take(j + 2)
+        row_ref[:, columns(j, width)] = jnp.dot(x_mate_ref[...], tile[...], preferred_element_type=f32).astype(bf16)
+        q_copy(j, core).start()
+        q_ref[:, columns(core * q_tiles + j, width)] = jnp.dot(x_ref[...], tile[...], preferred_element_type=f32).astype(bf16)
+
+        @pl.when(j >= 2)
+        def _():
+            kv_ring.step(j - 2)
+
     far = n // 4
-    for delta in range(kv_ring.len):
-        if delta != far:
+    ready = q_tiles - 2
+
+    def mate_keys(deltas):
+        for delta in deltas:
             for c in range(2):
                 kv_ring.wait_mate(delta, c)
+
+    mate_keys((0, 1, kv_ring.len - 1))
+
+    @pl.loop(0, q_tiles)
+    def _(j):
+        q_copy(j, 1 - core).wait_recv()
+        q_copy(j, core).wait_send()
+
+    x_copy.wait_send()
 
     per = rows // tok
     heads = q_ref.shape[1] // (kv_heads * HEAD_DIM)
@@ -260,6 +282,12 @@
     def _(i):
         attend(i, full, True)
 
+        @pl.when(i == 0)
+        def _():
+            for r in range(ready, kv_steps):
+                kv_ring.step(jnp.int32(r))
+            mate_keys([d for d in range(2, kv_ring.len - 1) if d != far])
+
         @pl.loop(0, full)
         def _(k):
             @pl.when((i == 0) & (k == full - 1))
@@ -287,6 +315,10 @@
         buf[me, j] = h
         row_ref[:, columns(j, width)] = h
         ring.send_own(j)
+
+        @pl.when(j >= chunks - 2)
+        def _():
+            ring.step(j - (chunks - 2))
 
     router_copy.wait()
     expert = lax.broadcasted_iota(jnp.int32, (n_exp, tok), 0)
@@ -321,11 +353,11 @@
         g = jnp.dot(h, tiles.take(ends[3] + 2 * j)[...], preferred_element_type=f32)
         u = jnp.dot(h, tiles.take(ends[3] + 2 * j + 1)[...], preferred_element_type=f32)
         act_ref[:, columns(j, width)] = (g * jax.nn.sigmoid(g) * u).astype(bf16)
-        ring.step(j + jnp.minimum(j, half))
-
-        @pl.when(j < half)
-        def _():
-            ring.step(2 * j + 1)
+        ring.step(2 + j + jnp.minimum(j, half - 1))
+
+        @pl.when(j < half - 1)
+        def _():
+            ring.step(2 * j + 3)
 
     @pl.loop(0, chunks)
     def _(j):
@@ -334,7 +366,7 @@
 
         @pl.when(lax.rem(j, 2) == 1)
         def _():
-            ring.step(chunks + half + j // 2)
+            ring.step(chunks + half + 1 + j // 2)
 
     kv_ring.drain()
     for i in range(1, n):
@@ -363,9 +395,9 @@
     length = n // 2
     near = 2 * far - 3
 
-    @pl.loop(0, chunks)
+    @pl.loop(0, chunks - 1)
     def _(k):
-        ring.step(2 * chunks + k)
+        ring.step(2 * chunks + 1 + k)
 
         @pl.when(k < near)
         def _():
@@ -404,6 +436,7 @@
     n_exp = w_router.shape[1]
     n_loc = n_exp // n
     all_rows = tok * q_width // width
+    half_tiles = q_width // (2 * width)
     vmem = pl.BlockSpec(memory_space=pltpu.VMEM)
     hbm = pl.BlockSpec(memory_space=pltpu.HBM)
     dma = pltpu.SemaphoreType.DMA
@@ -425,10 +458,11 @@
             pltpu.VMEM((tok, span), jnp.float32),
             pltpu.VMEM((n, 2 * n_loc, tok), jnp.float32),
             pltpu.VMEM((n, 2 * n_loc, tok), jnp.float32),
-            dma((depth,)), dma((1,)), dma((n,)), dma((n,)),
+            pltpu.VMEM((tok, hidden), jnp.bfloat16),
+            dma((depth,)), dma((1,)), dma((n,)), dma((n,)), dma((2,)), dma((half_tiles,)), dma((half_tiles,)),
         ] + ring_scratch(n, 2) + ring_scratch(n, chunks),
         cost_estimate=pl.CostEstimate(flops=2 * tok * weights, bytes_accessed=2 * weights, transcendentals=0),
-        compiler_params=pltpu.CompilerParams(vmem_limit_bytes=45 * 2 ** 20, collective_id=0, has_side_effects=True),
+        compiler_params=pltpu.CompilerParams(vmem_limit_bytes=46 * 2 ** 20, collective_id=0, has_side_effects=True),
         name='moe_block',
     )(tokens, ids, w_key, w_value, w_query, w_router, w_out, w_gate, w_up, w_down)
 

time: 162 us -> 161 us (level)
  no operation moved by 1% of the time
where the time goes in v7:
time: 161 us
  Pallas kernels  153 us (95%)
  local copies, waits for them, and re-layouts  7.13 us (4%)
    pallas_call x1, Pallas kernels, moe_block(): pl.pallas_call(functools.partial(block_body, n, cap, span, rows), out_sha...  153 us
    unnamed x2, local copies, waits for them, and re-layouts  7.13 us

profile of v7, /device:TPU:21, one launch (start us, length us, event | category | flops | bytes accessed | tf_op | source)
XLA Modules:
  0.0 160.9 jit_solution(10897805504271522084)
XLA Ops:
  0.6 153.1 %moe_block.1 = (bf16[128,4096]{1,0:T(8,128)(2,1)S(1)}, bf16[8,256,4096]{2,1,0:T(8,128)(2,1)S(1)}) custom-call(bf16[128,4096]{1,0:T(8,128)(2,1)} %x_ref.1, s32[8,128]{1,0:T(8,128)} %bitcast.1, bf16[4096,512]{1,0:T(8,128)(2,1)} %wk_ref.1, bf16[4096,512]{1,0:T(8,128)(2,1)} %wv_ref.1, bf16[4096,8192]{1,0:T(8,128)(2,1)} %wq_ref.1, bf16[4096,128]{1,0:T(8,128)(2,1)} %wr_ref.1, ...), custom_call_target="tpu_custom_call" | custom-call | flops 31138512896 | bytes 243269632 | tf_op jit(solution)/shard_map/moe_block/pallas_call | solution.py:444
  153.7 1.0 copy.14
  154.7 6.2 %copy.15 = bf16[8,256,4096]{2,1,0:T(8,128)(2,1)} copy(bf16[8,256,4096]{2,1,0:T(8,128)(2,1)S(1)} %get-tuple-element.3) | data formatting | bytes 33554432
